TPU v7x, 256 devices: a whole 4x4x8 slice. The times are simulated.
256 devices in a mesh: row: 8 (over x, core), col: 32 (over y, z).
Axes of the slice: x: 4, y: 4, z: 8, core: 2. Of those that a mesh axis runs over, the one named last changes fastest.
Arguments:
- matrix: float32 [2048, 65536], P('col', 'row'), may hold values from -6 to 6
- basis: float32 [65536, 512], P(('row', 'col')), may hold values from -0.0234375 to 0.0234375
Outputs:
- root: float32 [512, 512], P('row', 'col')
- right: float32 [2048, 512], P('col')
All inputs are finite; a program needn't handle non-finite values.
Results may differ from a plain program's by a relative error of at most 0.00018.
Values sent between devices are 32-bit elements; how exact they have to be, the bound alone decides.
A program may use at most 64 MiB of HBM per device.

v0:
```python
import jax
import jax.numpy as jnp
from jax import lax
from jax.sharding import PartitionSpec as P

ITERS = 8


def copy_for_each(value, axis):
    copies = jnp.broadcast_to(value, (lax.axis_size(axis), *value.shape))
    return lax.all_to_all(copies, axis, split_axis=0, concat_axis=0, tiled=True)


def over_copies(value, axis):
    return copy_for_each(value, axis).sum(axis=0)


def cut_along(value, dim, size):
    before, after = (value.shape[:dim], value.shape[dim + 1 :])
    return jnp.moveaxis(value.reshape(*before, size, -1, *after), dim, 0)


def summed_on_arrival(value, axis, dim):
    size = lax.axis_size(axis)
    tiles = lax.all_to_all(cut_along(value, dim, size), axis, 0, 0, tiled=True)
    return jnp.sum(tiles, axis=0)


def filled_up(lines, size):
    spare = -lines.shape[0] % size
    if not spare:
        return lines
    return jnp.concatenate([lines, jnp.zeros((spare, *lines.shape[1:]), lines.dtype)])


def joined_along(tiles, dim):
    lengths = list(tiles.shape[1:])
    lengths[dim] *= tiles.shape[0]
    return jnp.moveaxis(tiles, 0, dim).reshape(lengths)


def gather_directly(value, axis, dim):
    return joined_along(copy_for_each(value, axis), dim)


def sum_by_parts(value, axes):
    lines = value.reshape(-1, value.shape[-1])
    own = summed_on_arrival(filled_up(lines, lax.axis_size(axes)), axes, 0)
    whole = gather_directly(own, axes, 0)
    return whole[: len(lines)].reshape(value.shape)


def polar_steps(gram, width):
    highest = lax.Precision.HIGHEST
    scale = jnp.sqrt(jnp.sum(gram * gram) + 1e-06)
    ident = jnp.eye(width, dtype=jnp.float32)
    upper = gram / scale
    lower = ident
    for step in range(ITERS):
        middle = 0.5 * (3.0 * ident - jnp.dot(lower, upper, precision=highest))
        upper = jnp.dot(upper, middle, precision=highest)
        lower = jnp.dot(middle, lower, precision=highest)
    return (upper, lower, jnp.sqrt(scale))


def local(matrix, basis):
    highest = lax.Precision.HIGHEST
    width = basis.shape[1]
    nrow = lax.axis_size("row")
    ncol = lax.axis_size("col")
    partial_proj = lax.dot_general(
        lax.all_gather(basis, "col", axis=0, tiled=True),
        matrix,
        (((0,), (1,)), ((), ())),
        precision=highest,
    )
    proj = over_copies(partial_proj, "row")
    gram = sum_by_parts(jnp.dot(proj, proj.T, precision=highest), "col")
    upper, lower, root_scale = polar_steps(gram, width)
    right = jnp.dot(proj.T, lower, precision=highest) / root_scale
    root_full = upper * root_scale
    row_len = width // nrow
    col_len = width // ncol
    root = lax.dynamic_slice(
        root_full,
        (lax.axis_index("row") * row_len, lax.axis_index("col") * col_len),
        (row_len, col_len),
    )
    return (root, right)


def solution(mesh):
    return jax.shard_map(
        local,
        mesh=mesh,
        in_specs=(P("col", "row"), P(("row", "col"), None)),
        out_specs=(P("row", "col"), P("col", None)),
        check_vma=False,
    )
```

profile of v0, /device:TPU:32, one launch (start us, length us, event | category | flops | bytes accessed | tf_op | source)
XLA Modules:
  0.0 314.1 jit_solution(718308807394610721)
XLA Ops:
  7.9 143.3 %all-gather.2.cloned.1.call-done = f32[8192,512]{1,0:T(8,128)} async-done(((f32[256,512]{1,0:T(8,128)}), f32[8192,512]{1,0:T(8,128)}) %all-gather.2.cloned.1.call-update) | async-done | bytes 16777232 | tf_op jit(solution)/shard_map/all_gather | solution.py:72
  151.2 13.4 %fusion.11 = f32[512,64]{0,1:T(8,128)S(1)} fusion(f32[8192,512]{1,0:T(8,128)} %all-gather.2.cloned.1.call-done, f32[64,8192]{1,0:T(8,128)S(1)} %copy-done), kind=kOutput, calls=%fused_computation.24 | convolution fusion | flops 3221225472 | bytes 19005440 | tf_op jit(solution)/shard_map/dot_general | solution.py:71
  164.7 20.0 %all_to_all.15 = f32[8,512,64]{1,2,0:T(8,128)S(1)} all-to-all(f32[8,512,64]{1,2,0:T(8,128)S(1)} %broadcast_in_dim.6), channel_id=1, replica_groups=mesh['row'=8,'col'=32] {'row'}, dimensions={0} | all-to-all | bytes 2097152 | tf_op jit(solution)/shard_map/all_to_all | solution.py:11
  186.0 35.6 %all_to_all.16 = f32[32,16,512]{2,1,0:T(8,128)S(1)} all-to-all(f32[32,16,512]{2,1,0:T(8,128)S(1)} %fusion.9), channel_id=1, replica_groups=mesh['row'=8,'col'=32] {'col'}, dimensions={0} | all-to-all | bytes 2097152 | tf_op jit(solution)/shard_map/all_to_all | solution.py:25
  222.7 5.7 %all-to-all-start.2 = ((f32[32,16,512]{2,1,0:T(8,128)}), f32[32,16,512]{2,1,0:T(8,128)S(1)}, u32[]{:S(2)}, u32[]{:S(2)}) async-start(f32[32,16,512]{2,1,0:T(8,128)} %broadcast_in_dim.7), calls=%async_computation.2 | async-start | bytes 2097152 | tf_op jit(solution)/shard_map/all_to_all | solution.py:11
  228.4 27.5 %all-to-all-done.2 = f32[32,16,512]{2,1,0:T(8,128)S(1)} async-done(((f32[32,16,512]{2,1,0:T(8,128)}), f32[32,16,512]{2,1,0:T(8,128)S(1)}, u32[]{:S(2)}, u32[]{:S(2)}) %all-to-all-start.2) | async-done | bytes 1048608 | tf_op jit(solution)/shard_map/all_to_all | solution.py:11
  258.7 1.8 fusion.12
  261.6 1.9 fusion
  263.4 1.8 fusion.13
  267.1 1.8 fusion.1
  269.0 2.0 fusion.16
  271.0 1.8 fusion.15
  272.9 1.9 fusion.2
  274.7 1.8 fusion.18
  276.6 1.8 fusion.17
  278.4 1.8 fusion.3
  280.3 1.8 fusion.20
  282.2 2.1 fusion.19
  284.3 1.8 fusion.4
  286.1 1.8 fusion.22
  289.8 1.8 fusion.5
  293.5 2.8 fusion.23
  296.4 3.3 %fusion.6 = f32[512,512]{1,0:T(8,128)S(1)} fusion(f32[512,512]{1,0:T(8,128)S(1)} %fusion.24, f32[512,512]{1,0:T(8,128)} %fusion.23), kind=kOutput, calls=%fused_computation.14 | convolution fusion | flops 1611661312 | bytes 3145728 | tf_op jit(solution)/shard_map/dot_general | solution.py:60
  301.6 3.1 fusion.25
  (20 shorter events, 15.7 us)
Async XLA Ops:
  7.2 144.0 %copy-start = (f32[64,8192]{1,0:T(8,128)S(1)}, f32[64,8192]{1,0:T(8,128)}, u32[]{:S(2)}) copy-start(f32[64,8192]{1,0:T(8,128)} %param.2) | copy-start | bytes 6291460
  7.2 144.0 %all-gather.2.cloned.1.call-start = ((), (), s32[]{:S(2)}) async-start(), calls=%async_computation.3 | async-start | bytes 17301504 | tf_op jit(solution)/shard_map/all_gather | solution.py:72
  222.7 33.2 %all-to-all-start.2 = ((f32[32,16,512]{2,1,0:T(8,128)}), f32[32,16,512]{2,1,0:T(8,128)S(1)}, u32[]{:S(2)}, u32[]{:S(2)}) async-start(f32[32,16,512]{2,1,0:T(8,128)} %broadcast_in_dim.7), calls=%async_computation.2 | async-start | bytes 2097152 | tf_op jit(solution)/shard_map/all_to_all | solution.py:11
Sparse Core Ops, SparseCore 0:
  10.6 140.5 all-gather.1
where the time goes:
time: 319 us; the launch traced here: 314 us
  waiting for transfers between devices  171 us (54%)
  matrix products  62.7 us (20%)
  blocking collectives  55.6 us (17%)
  between operations  15.5 us (5%)
  starting transfers between devices  5.7 us (2%)
    all_gather x1, waiting for transfers between devices, local(): lax.all_gather(basis, 'col', axis=0, tiled=True)  143 us
    all_to_all x1, blocking collectives, summed_on_arrival(): tiles = lax.all_to_all(cut_along(value, dim, size), axis, 0, 0, tiled=True)  35.6 us
    all_to_all x1, waiting for transfers between devices, copy_for_each(): return lax.all_to_all(copies, axis, split_axis=0, concat_axis=0, tiled=True)  27.5 us
    all_to_all x1, blocking collectives, copy_for_each(): return lax.all_to_all(copies, axis, split_axis=0, concat_axis=0, tiled=True)  20 us
    dot_general x8, matrix products, polar_steps(): upper = jnp.dot(upper, middle, precision=highest)  17.2 us
    dot_general x8, matrix products, polar_steps(): middle = 0.5 * (3.0 * ident - jnp.dot(lower, upper, precision=highest))  15.5 us
    dot_general x8, matrix products, polar_steps(): lower = jnp.dot(middle, lower, precision=highest)  14.1 us
    dot_general x1, matrix products, local(): lax.dot_general(lax.all_gather(basis, 'col', axis=0, tiled=True), matrix,...  13.4 us
  transfers between devices with their start and end apart: 2, of which 2 were waited for; matrix products, arithmetic and copies ran while one was open for 0% of the time, Pallas kernels for 0%

commit v1 on v0

v1 whole, which is shorter than its diff:
```python
import functools

import jax
import jax.numpy as jnp
from jax import lax
from jax.experimental import pallas as pl
from jax.experimental.pallas import tpu as pltpu
from jax.sharding import PartitionSpec as P

MESH = pl.DeviceIdType.MESH
ITERS = 8
F32 = jnp.float32
BF16 = jnp.bfloat16
NX, NY, NZ = 4, 4, 8
NR, PLANE = 2 * NX, 2 * NX * NY


def split(a):
    hi = a.astype(BF16)
    return hi, (a - hi.astype(F32)).astype(BF16)


def product(ah, al, bh, bl, dims=(((1,), (0,)), ((), ()))):
    dot = functools.partial(
        lax.dot_general, dimension_numbers=dims, preferred_element_type=F32
    )
    return dot(ah, bh) + (dot(ah, bl) + dot(al, bh))


def lanes(i, size):
    return pl.ds(pl.multiple_of(i * size, size), size)


def gather_kernel(
    mat, bas, gram, own_cols,
    m_in, m_hi, m_lo, q, acc, land, proj, block, zland,
    y_send, y_recv, f_send, f_recv, b_send, b_recv, local_sem,
    p_send, p_recv, a_send, a_recv, z_send, z_recv, g_send, g_recv, d_send, d_recv,
):
    r, c = lax.axis_index("row"), lax.axis_index("col")
    y, z = c // NZ, c % NZ
    x, core = r // 2, r % 2
    cols = mat.shape[0]
    part = mat.shape[1] // NY
    rows, width = bas.shape
    half = rows // 2
    wide = width // 4
    piece = cols // NR

    def plane_peer(k):
        return (r + k // NY) % NR, (y + k % NY) % NY

    def z_peer(k):
        return (r, y * NZ + (z + k) % NZ)

    barrier = pltpu.get_barrier_semaphore()

    def greet_plane(k, _):
        r2, y2 = plane_peer(k)
        pl.semaphore_signal(barrier, inc=1, device_id=(r2, y2 * NZ + z), device_id_type=MESH)
        return 0

    def greet_z(k, _):
        pl.semaphore_signal(barrier, inc=1, device_id=z_peer(k), device_id_type=MESH)
        return 0

    lax.fori_loop(1, PLANE, greet_plane, 0)
    lax.fori_loop(1, NZ, greet_z, 0)
    pl.semaphore_wait(barrier, PLANE - 1 + NZ - 1)

    def ring_copy(m, d, ahead):
        sign = 1 if ahead else -1
        owner = (z - sign * d + NZ) % NZ
        here = pl.ds(m * wide, wide)
        if d == 0:
            src = bas.at[:, here]
            dst = q.at[lanes(owner, rows), here]
        else:
            span = pl.ds(pl.multiple_of(owner * rows, rows), rows)
            if d == 3:
                start = owner * rows + (0 if ahead else half)
                span = pl.ds(pl.multiple_of(start, half), half)
            src = dst = q.at[span, here]
        send, recv = (f_send, f_recv) if ahead else (b_send, b_recv)
        return pltpu.make_async_remote_copy(
            src_ref=src, dst_ref=dst, send_sem=send.at[m, d], recv_sem=recv.at[m, d],
            device_id=(r, y * NZ + (z + sign + NZ) % NZ), device_id_type=MESH,
        )

    def ring_wait(m, d, ahead):
        sign = 1 if ahead else -1
        owner = (z - sign * (d + 1) + NZ) % NZ
        here = pl.ds(m * wide, wide)
        span = pl.ds(pl.multiple_of(owner * rows, rows), rows)
        if d == 3:
            start = owner * rows + (0 if ahead else half)
            span = pl.ds(pl.multiple_of(start, half), half)
        send, recv = (f_send, f_recv) if ahead else (b_send, b_recv)
        pltpu.make_async_remote_copy(
            src_ref=q.at[span, here], dst_ref=q.at[span, here],
            send_sem=send.at[m, d], recv_sem=recv.at[m, d],
            device_id=(r, y * NZ + (z + sign + NZ) % NZ), device_id_type=MESH,
        ).wait_recv()

    def y_copy(k):
        y2 = (y + k) % NY
        return pltpu.make_async_remote_copy(
            src_ref=mat.at[:, lanes(y2, part)], dst_ref=m_in.at[lanes(y, cols), :],
            send_sem=y_send.at[k - 1], recv_sem=y_recv.at[k - 1],
            device_id=(r, y2 * NZ + z), device_id_type=MESH,
        )

    def y_wait(k):
        src = (y - k + NY) % NY
        pltpu.make_async_remote_copy(
            src_ref=mat.at[:, lanes(src, part)], dst_ref=m_in.at[lanes(src, cols), :],
            send_sem=y_send.at[k - 1], recv_sem=y_recv.at[k - 1],
            device_id=(r, src * NZ + z), device_id_type=MESH,
        ).wait_recv()

    copies = []

    def issue(m, d):
        for ahead in (True, False):
            if d > 0:
                ring_wait(m, d - 1, ahead)
            copy = ring_copy(m, d, ahead)
            copy.start()
            copies.append(copy)

    def split_rows(src):
        def one(i, _):
            at = pl.ds(pl.multiple_of(i * 16, 16), 16)
            hi, lo = split(m_in[at, :])
            m_hi[at, :] = hi
            m_lo[at, :] = lo
            return 0

        lax.fori_loop(src * (cols // 16), (src + 1) * (cols // 16), one, 0)

    def own_split(i, _):
        hi, lo = split(mat[pl.ds(pl.multiple_of(i * 16, 16), 16), lanes(y, part)])
        at = pl.ds(pl.multiple_of(y * cols + i * 16, 16), 16)
        m_hi[at, :] = hi
        m_lo[at, :] = lo
        return 0

    def multiply(pair, first, last):
        here = pl.ds(pair * 2 * wide, 2 * wide)

        def one(o, _):
            owner = (z + o) % NZ
            qh, ql = split(q[lanes(owner, rows), here])
            at = lanes(owner, rows)
            acc[:, here] += product(m_hi[:, at], m_lo[:, at], qh, ql)
            return 0

        lax.fori_loop(first, last, one, 0)

    def spread_partial(pair):
        here = pl.ds(pair * 2 * wide, 2 * wide)

        def one(k, _):
            r2, y2 = plane_peer(k)
            src = pl.ds(pl.multiple_of(y2 * cols + r2 * piece, piece), piece)
            pltpu.make_async_remote_copy(
                src_ref=acc.at[src, here], dst_ref=land.at[lanes(k - 1, piece), here],
                send_sem=p_send.at[pair], recv_sem=p_recv.at[pair],
                device_id=(r2, y2 * NZ + z), device_id_type=MESH,
            ).start()
            return 0

        lax.fori_loop(1, PLANE, one, 0)

    mine = pl.ds(pl.multiple_of(y * cols + r * piece, piece), piece)

    def all_of(ref, pair, send, recv):
        here = pl.ds(pair * 2 * wide, 2 * wide)
        view = ref.at[pl.ds(0, (PLANE - 1) * piece), here]
        return pltpu.make_async_remote_copy(
            src_ref=view, dst_ref=view, send_sem=send.at[pair], recv_sem=recv.at[pair],
            device_id=z_peer(1), device_id_type=MESH,
        )

    def total_and_spread(pair):
        here = pl.ds(pair * 2 * wide, 2 * wide)
        all_of(land, pair, p_send, p_recv).wait_recv()
        total = acc[mine, here]
        for k in range(PLANE - 1):
            total = total + land[pl.ds(k * piece, piece), here]
        proj[mine, here] = total

        def one(k, _):
            r2, y2 = plane_peer(k)
            pltpu.make_async_remote_copy(
                src_ref=proj.at[mine, here], dst_ref=proj.at[mine, here],
                send_sem=a_send.at[pair], recv_sem=a_recv.at[pair],
                device_id=(r2, y2 * NZ + z), device_id_type=MESH,
            ).start()
            return 0

        lax.fori_loop(1, PLANE, one, 0)

    own = pltpu.make_async_copy(bas, q.at[lanes(z, rows), :], local_sem)
    own.start()
    issue(0, 0)
    for k in range(1, NY):
        y_copy(k).start()
    issue(1, 0)
    acc[...] = jnp.zeros_like(acc)
    lax.fori_loop(0, cols // 16, own_split, 0)
    own.wait()
    for d in range(1, 4):
        issue(0, d)
        issue(1, d)
    issue(2, 0)
    issue(3, 0)
    issue(2, 1)
    issue(3, 1)
    issue(2, 2)
    for k in range(1, NY):
        y_wait(k)
        split_rows((y - k + NY) % NY)
    for m in (0, 1):
        for ahead in (True, False):
            ring_wait(m, 3, ahead)
    multiply(0, 0, NZ)
    spread_partial(0)
    issue(3, 2)
    multiply(1, 0, 3)
    issue(2, 3)
    issue(3, 3)
    multiply(1, 3, 4)
    multiply(1, 5, NZ)
    total_and_spread(0)
    for m in (2, 3):
        for ahead in (True, False):
            ring_wait(m, 3, ahead)
    multiply(1, 4, 5)
    spread_partial(1)
    total_and_spread(1)
    for pair in (0, 1):
        all_of(proj, pair, a_send, a_recv).wait_recv()
    own_cols[...] = proj[lanes(y, cols), :]

    side = width // 4
    lh, ll = split(proj[:, lanes(y, side)].T)
    rh, rl = split(proj[:, lanes(x, side)])
    block[...] = product(lh, ll, rh, rl)
    low = side // 2
    my_half = pl.ds(pl.multiple_of(core * low, low), low)
    zland[lanes(z, low), :] = block[my_half, :]

    def to_z(k, _):
        pltpu.make_async_remote_copy(
            src_ref=block.at[my_half, :], dst_ref=zland.at[lanes(z, low), :],
            send_sem=z_send, recv_sem=z_recv, device_id=z_peer(k), device_id_type=MESH,
        ).start()
        return 0

    lax.fori_loop(1, NZ, to_z, 0)
    view = zland.at[pl.ds(0, (NZ - 1) * low), :]
    z_all = pltpu.make_async_remote_copy(
        src_ref=view, dst_ref=view, send_sem=z_send, recv_sem=z_recv,
        device_id=z_peer(1), device_id_type=MESH,
    )
    z_all.wait_recv()
    total = zland[pl.ds(0, low), :]
    for k in range(1, NZ):
        total = total + zland[pl.ds(k * low, low), :]

    def gram_rows(y2):
        return pl.ds(pl.multiple_of(y2 * side + core * low, low), low)

    here = lanes(x, side)
    gram[gram_rows(y), here] = total
    for k in range(1, NX * NY):
        kx, ky = k % NX, k // NX
        r2 = ((x + kx) % NX) * 2 + core
        pltpu.make_async_remote_copy(
            src_ref=gram.at[gram_rows(y), here], dst_ref=gram.at[gram_rows(y), here],
            send_sem=g_send, recv_sem=g_recv.at[ky],
            device_id=(r2, ((y + ky) % NY) * NZ + z), device_id_type=MESH,
        ).start()
    partner = (x * 2 + 1 - core, c)
    crossings = []
    for ky in range(NY):
        y2 = (y - ky + NY) % NY
        count = (NX - 1 if ky == 0 else NX) * side
        view = gram.at[gram_rows(y2), pl.ds(0, count)]
        pltpu.make_async_remote_copy(
            src_ref=view, dst_ref=view, send_sem=g_send, recv_sem=g_recv.at[ky],
            device_id=partner, device_id_type=MESH,
        ).wait_recv()
        copy = pltpu.make_async_remote_copy(
            src_ref=gram.at[gram_rows(y2), :], dst_ref=gram.at[gram_rows(y2), :],
            send_sem=d_send.at[ky], recv_sem=d_recv.at[ky],
            device_id=partner, device_id_type=MESH,
        )
        copy.start()
        crossings.append(copy)
    for ky in range(NY):
        y2 = (y - ky + NY) % NY
        theirs = pl.ds(pl.multiple_of(y2 * side + (1 - core) * low, low), low)
        pltpu.make_async_remote_copy(
            src_ref=gram.at[theirs, :], dst_ref=gram.at[theirs, :],
            send_sem=d_send.at[ky], recv_sem=d_recv.at[ky],
            device_id=partner, device_id_type=MESH,
        ).wait_recv()

    for copy in copies + crossings:
        copy.wait_send()
    for k in range(1, NY):
        y_copy(k).wait_send()
    for pair in (0, 1):
        all_of(land, pair, p_send, p_recv).wait_send()
        all_of(proj, pair, a_send, a_recv).wait_send()
    z_all.wait_send()
    view = zland.at[pl.ds(0, low), :]
    for k in range(1, NX * NY):
        pltpu.make_async_remote_copy(
            src_ref=view, dst_ref=view, send_sem=g_send, recv_sem=g_recv.at[0],
            device_id=partner, device_id_type=MESH,
        ).wait_send()


def gather(matrix, basis):
    cols, depth = matrix.shape
    rows, width = basis.shape
    part = depth // NY
    side = width // 4
    dma = pltpu.SemaphoreType.DMA
    vmem = pl.BlockSpec(memory_space=pltpu.VMEM)
    return pl.pallas_call(
        gather_kernel,
        name="gather",
        out_shape=(
            jax.ShapeDtypeStruct((width, width), F32),
            jax.ShapeDtypeStruct((cols, width), F32),
        ),
        in_specs=[vmem, vmem],
        out_specs=(vmem, vmem),
        scratch_shapes=[
            pltpu.VMEM((NY * cols, part), F32),
            pltpu.VMEM((NY * cols, part), BF16),
            pltpu.VMEM((NY * cols, part), BF16),
            pltpu.VMEM((NZ * rows, width), F32),
            pltpu.VMEM((NY * cols, width), F32),
            pltpu.VMEM(((PLANE - 1) * cols // NR, width), F32),
            pltpu.VMEM((NY * cols, width), F32),
            pltpu.VMEM((side, side), F32),
            pltpu.VMEM((NZ * side // 2, side), F32),
            dma((NY - 1,)), dma((NY - 1,)),
            dma((4, 4)), dma((4, 4)), dma((4, 4)), dma((4, 4)), dma,
            dma((2,)), dma((2,)), dma((2,)), dma((2,)),
            dma, dma, dma, dma((NY,)), dma((NY,)), dma((NY,)),
        ],
        compiler_params=pltpu.CompilerParams(
            collective_id=0, has_side_effects=True, vmem_limit_bytes=48 * 2**20
        ),
    )(matrix, basis)


def polar_kernel(gram, own_cols, root, right, t, t_hi, t_lo, b_hi, b_lo, v):
    r, c = lax.axis_index("row"), lax.axis_index("col")
    width = gram.shape[0]
    cols = own_cols.shape[0]
    row_len = root.shape[0]
    total = jnp.sum(gram[...] * gram[...])
    scale = jnp.sqrt(jnp.full((1, 1), total, F32) + 1e-06)
    root_scale = jnp.sqrt(scale)
    t[...] = gram[...] / scale
    v[pl.ds(0, cols), :] = own_cols[...]
    v[pl.ds(cols, row_len), :] = gram[lanes(r, row_len), :] / scale

    def split_t():
        hi, lo = split(t[...])
        t_hi[...] = hi
        t_lo[...] = lo

    def advance():
        vh, vl = split(v[...])
        v[...] = 1.5 * v[...] - 0.5 * product(vh, vl, t_hi[...], t_lo[...])

    def step(_, carry):
        split_t()
        advance()
        b = product(t_hi[...], t_lo[...], t_hi[...], t_lo[...])
        hi, lo = split(b)
        b_hi[...] = hi
        b_lo[...] = lo
        t[...] = (2.25 * t[...] - 1.5 * b) + 0.25 * product(
            b_hi[...], b_lo[...], t_hi[...], t_lo[...]
        )
        return carry

    lax.fori_loop(0, ITERS - 1, step, 0)
    split_t()
    advance()
    right[...] = v[pl.ds(0, cols), :] / root_scale
    ours = v[pl.ds(cols, row_len), :] * root_scale
    col_len = root.shape[1]
    turn = (width - c * col_len) % width
    root[...] = pltpu.roll(ours, turn, 1)[:, :col_len]


def polar(gram, own_cols, row_len, col_len):
    width = gram.shape[0]
    cols = own_cols.shape[0]
    vmem = pl.BlockSpec(memory_space=pltpu.VMEM)
    return pl.pallas_call(
        polar_kernel,
        name="polar",
        out_shape=(
            jax.ShapeDtypeStruct((row_len, col_len), F32),
            jax.ShapeDtypeStruct((cols, width), F32),
        ),
        in_specs=[vmem, vmem],
        out_specs=(vmem, vmem),
        scratch_shapes=[
            pltpu.VMEM((width, width), F32),
            pltpu.VMEM((width, width), BF16),
            pltpu.VMEM((width, width), BF16),
            pltpu.VMEM((width, width), BF16),
            pltpu.VMEM((width, width), BF16),
            pltpu.VMEM((cols + row_len, width), F32),
        ],
    )(gram, own_cols)


def local(matrix, basis):
    width = basis.shape[1]
    gram, own_cols = gather(matrix, basis)
    return polar(
        gram, own_cols, width // lax.axis_size("row"), width // lax.axis_size("col")
    )


def solution(mesh):
    return jax.shard_map(
        local,
        mesh=mesh,
        in_specs=(P("col", "row"), P(("row", "col"), None)),
        out_specs=(P("row", "col"), P("col", None)),
        check_vma=False,
    )
```

time: 319 us -> 112 us (0.35)
  the two profiles are of different devices: /device:TPU:32 before, /device:TPU:1 now
where the time goes in v1:
time: 112 us
  Pallas kernels  105 us (94%)
  local copies, waits for them, and re-layouts  5.66 us (5%)
    pallas_call x1, Pallas kernels, gather(): pl.pallas_call(gather_kernel, name='gather', out_shape=(jax.ShapeDtypeStr...  87.4 us
    pallas_call x1, Pallas kernels, polar(): pl.pallas_call(polar_kernel, name='polar', out_shape=(jax.ShapeDtypeStruc...  18 us
    unnamed x8, local copies, waits for them, and re-layouts  4.23 us

profile of v1, /device:TPU:1, one launch (start us, length us, event | category | flops | bytes accessed | tf_op | source)
XLA Modules:
  0.0 111.6 jit_solution(2705354872361833609)
XLA Ops:
  0.6 0.0 copy-start
  0.6 1.6 %copy-done = f32[64,8192]{1,0:T(8,128)S(1)} copy-done((f32[64,8192]{1,0:T(8,128)S(1)}, f32[64,8192]{1,0:T(8,128)}, u32[]{:S(2)}) %copy-start) | copy-done | bytes 2097176
  2.2 0.0 copy-start.2
  2.2 1.0 copy-done.2
  3.3 87.4 %gather.1 = (f32[512,512]{1,0:T(8,128)S(1)}, f32[64,512]{1,0:T(8,128)S(1)}) custom-call(f32[64,8192]{1,0:T(8,128)S(1)} %copy-done, f32[256,512]{1,0:T(8,128)S(1)} %copy-done.2), custom_call_target="tpu_custom_call" | custom-call | tf_op jit(solution)/shard_map/gather/pallas_call | solution.py:334
  90.6 0.0 copy-start.1
  90.6 1.0 copy-done.1
  91.6 0.0 copy-start.3
  91.6 0.6 copy-done.3
  92.2 18.0 %polar.1 = (f32[64,16]{1,0:T(8,128)}, f32[64,512]{1,0:T(8,128)}) custom-call(f32[512,512]{1,0:T(8,128)} %copy-done.1, f32[64,512]{1,0:T(8,128)} %copy-done.3), custom_call_target="tpu_custom_call" | custom-call | tf_op jit(solution)/shard_map/polar/pallas_call | solution.py:411
  110.2 1.4 %copy.4 = f32[64,16]{0,1:T(8,128)} copy(f32[64,16]{1,0:T(8,128)} %get-tuple-element.6) | data formatting | bytes 8192 | tf_op jit(solution)/shard_map/polar/pallas_call | solution.py:411
Async XLA Ops:
  0.6 1.6 %copy-start = (f32[64,8192]{1,0:T(8,128)S(1)}, f32[64,8192]{1,0:T(8,128)}, u32[]{:S(2)}) copy-start(f32[64,8192]{1,0:T(8,128)} %mat.1) | copy-start | bytes 6291460
  2.2 1.0 copy-start.2
  90.6 1.0 copy-start.1
  91.6 0.6 copy-start.3

commit v2 on v1

--- a/solution.py
+++ b/solution.py
@@ -31,9 +31,10 @@
     return pl.ds(pl.multiple_of(i * size, size), size)
 
 
-def gather_kernel(
-    mat, bas, gram, own_cols,
-    m_in, m_hi, m_lo, q, acc, land, proj, block, zland,
+def step_kernel(
+    mat_hbm, bas_hbm, root, right,
+    mat, m_in, m_hi, m_lo, q, acc, land, proj, block, own_piece, zland, packed,
+    t, t_hi, t_lo, b_hi, b_lo, v,
     y_send, y_recv, f_send, f_recv, b_send, b_recv, local_sem,
     p_send, p_recv, a_send, a_recv, z_send, z_recv, g_send, g_recv, d_send, d_recv,
 ):
@@ -42,7 +43,7 @@
     x, core = r // 2, r % 2
     cols = mat.shape[0]
     part = mat.shape[1] // NY
-    rows, width = bas.shape
+    rows, width = bas_hbm.shape
     half = rows // 2
     wide = width // 4
     piece = cols // NR
@@ -52,6 +53,11 @@
 
     def z_peer(k):
         return (r, y * NZ + (z + k) % NZ)
+
+    own_basis = pltpu.make_async_copy(bas_hbm, q.at[lanes(z, rows), :], local_sem.at[0])
+    own_basis.start()
+    own_matrix = pltpu.make_async_copy(mat_hbm, mat, local_sem.at[1])
+    own_matrix.start()
 
     barrier = pltpu.get_barrier_semaphore()
 
@@ -72,18 +78,13 @@
         sign = 1 if ahead else -1
         owner = (z - sign * d + NZ) % NZ
         here = pl.ds(m * wide, wide)
-        if d == 0:
-            src = bas.at[:, here]
-            dst = q.at[lanes(owner, rows), here]
-        else:
-            span = pl.ds(pl.multiple_of(owner * rows, rows), rows)
-            if d == 3:
-                start = owner * rows + (0 if ahead else half)
-                span = pl.ds(pl.multiple_of(start, half), half)
-            src = dst = q.at[span, here]
+        span = pl.ds(pl.multiple_of(owner * rows, rows), rows)
+        if d == 3:
+            start = owner * rows + (0 if ahead else half)
+            span = pl.ds(pl.multiple_of(start, half), half)
         send, recv = (f_send, f_recv) if ahead else (b_send, b_recv)
         return pltpu.make_async_remote_copy(
-            src_ref=src, dst_ref=dst, send_sem=send.at[m, d], recv_sem=recv.at[m, d],
+            src_ref=q.at[span, here], dst_ref=q.at[span, here], send_sem=send.at[m, d], recv_sem=recv.at[m, d],
             device_id=(r, y * NZ + (z + sign + NZ) % NZ), device_id_type=MESH,
         )
 
@@ -201,15 +202,14 @@
 
         lax.fori_loop(1, PLANE, one, 0)
 
-    own = pltpu.make_async_copy(bas, q.at[lanes(z, rows), :], local_sem)
-    own.start()
+    own_basis.wait()
     issue(0, 0)
+    own_matrix.wait()
     for k in range(1, NY):
         y_copy(k).start()
     issue(1, 0)
     acc[...] = jnp.zeros_like(acc)
     lax.fori_loop(0, cols // 16, own_split, 0)
-    own.wait()
     for d in range(1, 4):
         issue(0, d)
         issue(1, d)
@@ -241,44 +241,54 @@
     total_and_spread(1)
     for pair in (0, 1):
         all_of(proj, pair, a_send, a_recv).wait_recv()
-    own_cols[...] = proj[lanes(y, cols), :]
-
-    side = width // 4
-    lh, ll = split(proj[:, lanes(y, side)].T)
-    rh, rl = split(proj[:, lanes(x, side)])
-    block[...] = product(lh, ll, rh, rl)
+
+    side = width // NY
     low = side // 2
-    my_half = pl.ds(pl.multiple_of(core * low, low), low)
-    zland[lanes(z, low), :] = block[my_half, :]
+    tile = 8
+    s = y * NX + x
+    count = 10 * low // tile // (NX * NY)
+    first = s * count // (low // tile)
+    for n in range(2):
+        b = (first + n) % 10
+        i = b % NY
+        lh, ll = split(proj[:, lanes(i, side)].T)
+        rh, rl = split(proj[:, lanes((i + b // NY) % NY, side)])
+        block[pl.ds(n * side, side), :] = product(lh, ll, rh, rl)
+    for n in range(count):
+        at = s * count + n
+        row = (at // (low // tile) - first) * side + core * low + at % (low // tile) * tile
+        own_piece[pl.ds(n * tile, tile), :] = block[pl.ds(pl.multiple_of(row, tile), tile), :]
+    size = count * tile
+    zland[lanes(z, size), :] = own_piece[...]
 
     def to_z(k, _):
         pltpu.make_async_remote_copy(
-            src_ref=block.at[my_half, :], dst_ref=zland.at[lanes(z, low), :],
+            src_ref=own_piece, dst_ref=zland.at[lanes(z, size), :],
             send_sem=z_send, recv_sem=z_recv, device_id=z_peer(k), device_id_type=MESH,
         ).start()
         return 0
 
     lax.fori_loop(1, NZ, to_z, 0)
-    view = zland.at[pl.ds(0, (NZ - 1) * low), :]
+    view = zland.at[pl.ds(0, (NZ - 1) * size), :]
     z_all = pltpu.make_async_remote_copy(
         src_ref=view, dst_ref=view, send_sem=z_send, recv_sem=z_recv,
         device_id=z_peer(1), device_id_type=MESH,
     )
     z_all.wait_recv()
-    total = zland[pl.ds(0, low), :]
+    total = zland[pl.ds(0, size), :]
     for k in range(1, NZ):
-        total = total + zland[pl.ds(k * low, low), :]
-
-    def gram_rows(y2):
-        return pl.ds(pl.multiple_of(y2 * side + core * low, low), low)
-
-    here = lanes(x, side)
-    gram[gram_rows(y), here] = total
+        total = total + zland[pl.ds(k * size, size), :]
+
+    def packed_rows(of_core, of_y, of_x, chips):
+        return pl.ds(pl.multiple_of(((of_core * NY + of_y) * NX + of_x) * size, size), chips * size)
+
+    mine = packed_rows(core, y, x, 1)
+    packed[mine, :] = total
     for k in range(1, NX * NY):
         kx, ky = k % NX, k // NX
         r2 = ((x + kx) % NX) * 2 + core
         pltpu.make_async_remote_copy(
-            src_ref=gram.at[gram_rows(y), here], dst_ref=gram.at[gram_rows(y), here],
+            src_ref=packed.at[mine, :], dst_ref=packed.at[mine, :],
             send_sem=g_send, recv_sem=g_recv.at[ky],
             device_id=(r2, ((y + ky) % NY) * NZ + z), device_id_type=MESH,
         ).start()
@@ -286,92 +296,46 @@
     crossings = []
     for ky in range(NY):
         y2 = (y - ky + NY) % NY
-        count = (NX - 1 if ky == 0 else NX) * side
-        view = gram.at[gram_rows(y2), pl.ds(0, count)]
+        view = packed.at[pl.ds(0, (NX - 1 if ky == 0 else NX) * size), :]
         pltpu.make_async_remote_copy(
             src_ref=view, dst_ref=view, send_sem=g_send, recv_sem=g_recv.at[ky],
             device_id=partner, device_id_type=MESH,
         ).wait_recv()
+        at = packed_rows(core, y2, 0, NX)
         copy = pltpu.make_async_remote_copy(
-            src_ref=gram.at[gram_rows(y2), :], dst_ref=gram.at[gram_rows(y2), :],
+            src_ref=packed.at[at, :], dst_ref=packed.at[at, :],
             send_sem=d_send.at[ky], recv_sem=d_recv.at[ky],
             device_id=partner, device_id_type=MESH,
         )
         copy.start()
         crossings.append(copy)
     for ky in range(NY):
-        y2 = (y - ky + NY) % NY
-        theirs = pl.ds(pl.multiple_of(y2 * side + (1 - core) * low, low), low)
-        pltpu.make_async_remote_copy(
-            src_ref=gram.at[theirs, :], dst_ref=gram.at[theirs, :],
+        at = packed_rows(1 - core, (y - ky + NY) % NY, 0, NX)
+        pltpu.make_async_remote_copy(
+            src_ref=packed.at[at, :], dst_ref=packed.at[at, :],
             send_sem=d_send.at[ky], recv_sem=d_recv.at[ky],
             device_id=partner, device_id_type=MESH,
         ).wait_recv()
 
-    for copy in copies + crossings:
-        copy.wait_send()
-    for k in range(1, NY):
-        y_copy(k).wait_send()
-    for pair in (0, 1):
-        all_of(land, pair, p_send, p_recv).wait_send()
-        all_of(proj, pair, a_send, a_recv).wait_send()
-    z_all.wait_send()
-    view = zland.at[pl.ds(0, low), :]
-    for k in range(1, NX * NY):
-        pltpu.make_async_remote_copy(
-            src_ref=view, dst_ref=view, send_sem=g_send, recv_sem=g_recv.at[0],
-            device_id=partner, device_id_type=MESH,
-        ).wait_send()
-
-
-def gather(matrix, basis):
-    cols, depth = matrix.shape
-    rows, width = basis.shape
-    part = depth // NY
-    side = width // 4
-    dma = pltpu.SemaphoreType.DMA
-    vmem = pl.BlockSpec(memory_space=pltpu.VMEM)
-    return pl.pallas_call(
-        gather_kernel,
-        name="gather",
-        out_shape=(
-            jax.ShapeDtypeStruct((width, width), F32),
-            jax.ShapeDtypeStruct((cols, width), F32),
-        ),
-        in_specs=[vmem, vmem],
-        out_specs=(vmem, vmem),
-        scratch_shapes=[
-            pltpu.VMEM((NY * cols, part), F32),
-            pltpu.VMEM((NY * cols, part), BF16),
-            pltpu.VMEM((NY * cols, part), BF16),
-            pltpu.VMEM((NZ * rows, width), F32),
-            pltpu.VMEM((NY * cols, width), F32),
-            pltpu.VMEM(((PLANE - 1) * cols // NR, width), F32),
-            pltpu.VMEM((NY * cols, width), F32),
-            pltpu.VMEM((side, side), F32),
-            pltpu.VMEM((NZ * side // 2, side), F32),
-            dma((NY - 1,)), dma((NY - 1,)),
-            dma((4, 4)), dma((4, 4)), dma((4, 4)), dma((4, 4)), dma,
-            dma((2,)), dma((2,)), dma((2,)), dma((2,)),
-            dma, dma, dma, dma((NY,)), dma((NY,)), dma((NY,)),
-        ],
-        compiler_params=pltpu.CompilerParams(
-            collective_id=0, has_side_effects=True, vmem_limit_bytes=48 * 2**20
-        ),
-    )(matrix, basis)
-
-
-def polar_kernel(gram, own_cols, root, right, t, t_hi, t_lo, b_hi, b_lo, v):
-    r, c = lax.axis_index("row"), lax.axis_index("col")
-    width = gram.shape[0]
-    cols = own_cols.shape[0]
-    row_len = root.shape[0]
-    total = jnp.sum(gram[...] * gram[...])
-    scale = jnp.sqrt(jnp.full((1, 1), total, F32) + 1e-06)
+    squares = jnp.zeros((low, side), F32)
+    for b in range(10):
+        o, i = b // NY, b % NY
+        j = (i + o) % NY
+        for h in range(2):
+            part_of = packed[pl.ds((h * 10 + b) * low, low), :]
+            squares = squares + (1.0 if o == 0 else 2.0) * (part_of * part_of)
+            t[pl.ds(i * side + h * low, low), pl.ds(j * side, side)] = part_of
+        if o:
+            t[pl.ds(j * side, side), pl.ds(i * side, side)] = t[
+                pl.ds(i * side, side), pl.ds(j * side, side)
+            ].T
+    scale = jnp.sqrt(jnp.full((1, 1), jnp.sum(squares), F32) + 1e-06)
     root_scale = jnp.sqrt(scale)
-    t[...] = gram[...] / scale
-    v[pl.ds(0, cols), :] = own_cols[...]
-    v[pl.ds(cols, row_len), :] = gram[lanes(r, row_len), :] / scale
+    t[...] = t[...] / scale
+
+    wide_len, col_len = root.shape[1], root.shape[0]
+    v[pl.ds(0, cols), :] = proj[lanes(y, cols), :]
+    v[pl.ds(cols, col_len), :] = t[lanes(c, col_len), :]
 
     def split_t():
         hi, lo = split(t[...])
@@ -398,42 +362,74 @@
     split_t()
     advance()
     right[...] = v[pl.ds(0, cols), :] / root_scale
-    ours = v[pl.ds(cols, row_len), :] * root_scale
-    col_len = root.shape[1]
-    turn = (width - c * col_len) % width
-    root[...] = pltpu.roll(ours, turn, 1)[:, :col_len]
-
-
-def polar(gram, own_cols, row_len, col_len):
-    width = gram.shape[0]
-    cols = own_cols.shape[0]
+    ours = v[pl.ds(cols, col_len), :] * root_scale
+    turn = (width - r * wide_len) % width
+    root[...] = pltpu.roll(ours, turn, 1)[:, :wide_len]
+
+    for copy in copies + crossings:
+        copy.wait_send()
+    for k in range(1, NY):
+        y_copy(k).wait_send()
+    for pair in (0, 1):
+        all_of(land, pair, p_send, p_recv).wait_send()
+        all_of(proj, pair, a_send, a_recv).wait_send()
+    z_all.wait_send()
+    view = zland.at[pl.ds(0, size), :]
+    for k in range(1, NX * NY):
+        pltpu.make_async_remote_copy(
+            src_ref=view, dst_ref=view, send_sem=g_send, recv_sem=g_recv.at[0],
+            device_id=partner, device_id_type=MESH,
+        ).wait_send()
+
+
+def local(matrix, basis):
+    cols, depth = matrix.shape
+    rows, width = basis.shape
+    part = depth // NY
+    side = width // NY
+    size = 10 * side // (2 * NX * NY)
+    row_len, col_len = width // NR, width // (NY * NZ)
+    dma = pltpu.SemaphoreType.DMA
     vmem = pl.BlockSpec(memory_space=pltpu.VMEM)
-    return pl.pallas_call(
-        polar_kernel,
-        name="polar",
+    hbm = pl.BlockSpec(memory_space=pltpu.HBM)
+    root, right = pl.pallas_call(
+        step_kernel,
+        name="step",
         out_shape=(
-            jax.ShapeDtypeStruct((row_len, col_len), F32),
+            jax.ShapeDtypeStruct((col_len, row_len), F32),
             jax.ShapeDtypeStruct((cols, width), F32),
         ),
-        in_specs=[vmem, vmem],
+        in_specs=[hbm, hbm],
         out_specs=(vmem, vmem),
         scratch_shapes=[
+            pltpu.VMEM((cols, depth), F32),
+            pltpu.VMEM((NY * cols, part), F32),
+            pltpu.VMEM((NY * cols, part), BF16),
+            pltpu.VMEM((NY * cols, part), BF16),
+            pltpu.VMEM((NZ * rows, width), F32),
+            pltpu.VMEM((NY * cols, width), F32),
+            pltpu.VMEM(((PLANE - 1) * cols // NR, width), F32),
+            pltpu.VMEM((NY * cols, width), F32),
+            pltpu.VMEM((2 * side, side), F32),
+            pltpu.VMEM((size, side), F32),
+            pltpu.VMEM((NZ * size, side), F32),
+            pltpu.VMEM((PLANE * size, side), F32),
             pltpu.VMEM((width, width), F32),
             pltpu.VMEM((width, width), BF16),
             pltpu.VMEM((width, width), BF16),
             pltpu.VMEM((width, width), BF16),
             pltpu.VMEM((width, width), BF16),
-            pltpu.VMEM((cols + row_len, width), F32),
+            pltpu.VMEM((cols + col_len, width), F32),
+            dma((NY - 1,)), dma((NY - 1,)),
+            dma((4, 4)), dma((4, 4)), dma((4, 4)), dma((4, 4)), dma((2,)),
+            dma((2,)), dma((2,)), dma((2,)), dma((2,)),
+            dma, dma, dma, dma((NY,)), dma((NY,)), dma((NY,)),
         ],
-    )(gram, own_cols)
-
-
-def local(matrix, basis):
-    width = basis.shape[1]
-    gram, own_cols = gather(matrix, basis)
-    return polar(
-        gram, own_cols, width // lax.axis_size("row"), width // lax.axis_size("col")
-    )
+        compiler_params=pltpu.CompilerParams(
+            collective_id=0, has_side_effects=True, vmem_limit_bytes=60 * 2**20
+        ),
+    )(matrix, basis)
+    return root.T, right
 
 
 def solution(mesh):

time: 112 us -> 104 us (0.929)
  Pallas kernels: 105 us -> 101 us
  local copies, waits for them, and re-layouts: 5.66 us -> 2.86 us
    pallas_call x2 -> x1, Pallas kernels: 105 us -> 101 us  [local(): pl.pallas_call(step_kernel, name='step', out_shape=(jax.ShapeDtypeStruct(...]
    pallas_call x1 -> x0, local copies, waits for them, and re-layouts: 1.43 us -> none  [polar(): pl.pallas_call(polar_kernel, name='polar', out_shape=(jax.ShapeDtypeStruc...]
    unnamed x8 -> x2, local copies, waits for them, and re-layouts: 4.23 us -> 2.86 us
where the time goes in v2:
time: 104 us
  Pallas kernels  101 us (97%)
  local copies, waits for them, and re-layouts  2.86 us (3%)
    pallas_call x1, Pallas kernels, local(): pl.pallas_call(step_kernel, name='step', out_shape=(jax.ShapeDtypeStruct(...  101 us
    unnamed x2, local copies, waits for them, and re-layouts  2.86 us

profile of v2, /device:TPU:1, one launch (start us, length us, event | category | flops | bytes accessed | tf_op | source)
XLA Modules:
  0.0 104.0 jit_solution(4490763328669054702)
XLA Ops:
  0.6 100.5 %step.1 = (f32[16,64]{1,0:T(8,128)}, f32[64,512]{1,0:T(8,128)}) custom-call(f32[64,8192]{1,0:T(8,128)} %mat_hbm.1, f32[256,512]{1,0:T(8,128)} %bas_hbm.1), custom_call_target="tpu_custom_call" | custom-call | tf_op jit(solution)/shard_map/step/pallas_call | solution.py:395
  101.2 1.3 %copy.6 = f32[64,16]{0,1:T(8,128)} copy(f32[64,16]{0,1:T(8,128)} %bitcast.1) | data formatting | bytes 8192
  102.5 1.6 %copy.7 = f32[64,512]{1,0:T(8,128)} copy(f32[64,512]{1,0:T(8,128)} %get-tuple-element.9) | data formatting | bytes 262144

commit v3 on v2

--- a/solution.py
+++ b/solution.py
@@ -27,14 +27,20 @@
     return dot(ah, bh) + (dot(ah, bl) + dot(al, bh))
 
 
+PEERS = sorted(
+    [(dx, dy, dc) for dx in range(NX) for dy in range(NY) for dc in range(2)][1:],
+    key=lambda p: -(min(p[0], NX - p[0]) * 2 + min(p[1], NY - p[1]) * 2 + p[2]),
+)
+Z_STEPS = sorted(range(1, NZ), key=lambda d: -min(d, NZ - d))
+
+
 def lanes(i, size):
     return pl.ds(pl.multiple_of(i * size, size), size)
 
 
-def step_kernel(
-    mat_hbm, bas_hbm, root, right,
-    mat, m_in, m_hi, m_lo, q, acc, land, proj, block, own_piece, zland, packed,
-    t, t_hi, t_lo, b_hi, b_lo, v,
+def gather_kernel(
+    mat_hbm, bas_hbm, packed, own_cols,
+    mat, m_in, m_hi, m_lo, q, acc, land, proj, block, own_piece, zland,
     y_send, y_recv, f_send, f_recv, b_send, b_recv, local_sem,
     p_send, p_recv, a_send, a_recv, z_send, z_recv, g_send, g_recv, d_send, d_recv,
 ):
@@ -48,8 +54,14 @@
     wide = width // 4
     piece = cols // NR
 
+    near_x = [(x + d) % NX for d in range(NX)]
+    near_y = [(y + d) % NY for d in range(NY)]
+    near_row = [[n * 2 + (core + d) % 2 for d in range(2)] for n in near_x]
+    near_col = [n * NZ + z for n in near_y]
+
     def plane_peer(k):
-        return (r + k // NY) % NR, (y + k % NY) % NY
+        dx, dy, dc = PEERS[k]
+        return near_row[dx][dc], near_y[dy], near_col[dy]
 
     def z_peer(k):
         return (r, y * NZ + (z + k) % NZ)
@@ -61,18 +73,13 @@
 
     barrier = pltpu.get_barrier_semaphore()
 
-    def greet_plane(k, _):
-        r2, y2 = plane_peer(k)
-        pl.semaphore_signal(barrier, inc=1, device_id=(r2, y2 * NZ + z), device_id_type=MESH)
-        return 0
-
-    def greet_z(k, _):
+    for k in Z_STEPS:
         pl.semaphore_signal(barrier, inc=1, device_id=z_peer(k), device_id_type=MESH)
-        return 0
-
-    lax.fori_loop(1, PLANE, greet_plane, 0)
-    lax.fori_loop(1, NZ, greet_z, 0)
-    pl.semaphore_wait(barrier, PLANE - 1 + NZ - 1)
+    for k in range(PLANE - 1):
+        r2, _, c2 = plane_peer(k)
+        pl.semaphore_signal(barrier, inc=1, device_id=(r2, c2), device_id_type=MESH)
+    with jax.named_scope("barrier"):
+        pl.semaphore_wait(barrier, PLANE - 1 + NZ - 1)
 
     def ring_copy(m, d, ahead):
         sign = 1 if ahead else -1
@@ -161,17 +168,14 @@
     def spread_partial(pair):
         here = pl.ds(pair * 2 * wide, 2 * wide)
 
-        def one(k, _):
-            r2, y2 = plane_peer(k)
+        for k in range(PLANE - 1):
+            r2, y2, c2 = plane_peer(k)
             src = pl.ds(pl.multiple_of(y2 * cols + r2 * piece, piece), piece)
             pltpu.make_async_remote_copy(
-                src_ref=acc.at[src, here], dst_ref=land.at[lanes(k - 1, piece), here],
+                src_ref=acc.at[src, here], dst_ref=land.at[pl.ds(k * piece, piece), here],
                 send_sem=p_send.at[pair], recv_sem=p_recv.at[pair],
-                device_id=(r2, y2 * NZ + z), device_id_type=MESH,
+                device_id=(r2, c2), device_id_type=MESH,
             ).start()
-            return 0
-
-        lax.fori_loop(1, PLANE, one, 0)
 
     mine = pl.ds(pl.multiple_of(y * cols + r * piece, piece), piece)
 
@@ -191,16 +195,13 @@
             total = total + land[pl.ds(k * piece, piece), here]
         proj[mine, here] = total
 
-        def one(k, _):
-            r2, y2 = plane_peer(k)
+        for k in range(PLANE - 1):
+            r2, _, c2 = plane_peer(k)
             pltpu.make_async_remote_copy(
                 src_ref=proj.at[mine, here], dst_ref=proj.at[mine, here],
                 send_sem=a_send.at[pair], recv_sem=a_recv.at[pair],
-                device_id=(r2, y2 * NZ + z), device_id_type=MESH,
+                device_id=(r2, c2), device_id_type=MESH,
             ).start()
-            return 0
-
-        lax.fori_loop(1, PLANE, one, 0)
 
     own_basis.wait()
     issue(0, 0)
@@ -211,36 +212,55 @@
     acc[...] = jnp.zeros_like(acc)
     lax.fori_loop(0, cols // 16, own_split, 0)
     for d in range(1, 4):
-        issue(0, d)
-        issue(1, d)
-    issue(2, 0)
-    issue(3, 0)
-    issue(2, 1)
-    issue(3, 1)
-    issue(2, 2)
-    for k in range(1, NY):
-        y_wait(k)
-        split_rows((y - k + NY) % NY)
+        with jax.named_scope(f"issue_0{d}"):
+            issue(0, d)
+        with jax.named_scope(f"issue_1{d}"):
+            issue(1, d)
+    with jax.named_scope("issue_20"):
+        issue(2, 0)
+    with jax.named_scope("issue_30"):
+        issue(3, 0)
+    with jax.named_scope("issue_21"):
+        issue(2, 1)
+    with jax.named_scope("y_wait"):
+        for k in range(1, NY):
+            y_wait(k)
+            split_rows((y - k + NY) % NY)
     for m in (0, 1):
         for ahead in (True, False):
             ring_wait(m, 3, ahead)
-    multiply(0, 0, NZ)
-    spread_partial(0)
-    issue(3, 2)
+    with jax.named_scope("multiply_0"):
+        multiply(0, 0, NZ)
+    with jax.named_scope("spread_0"):
+        spread_partial(0)
+    with jax.named_scope("issue_31"):
+        issue(3, 1)
+    with jax.named_scope("issue_22"):
+        issue(2, 2)
+    with jax.named_scope("issue_32"):
+        issue(3, 2)
     multiply(1, 0, 3)
-    issue(2, 3)
-    issue(3, 3)
+    with jax.named_scope("issue_23"):
+        issue(2, 3)
+    with jax.named_scope("issue_33"):
+        issue(3, 3)
     multiply(1, 3, 4)
     multiply(1, 5, NZ)
-    total_and_spread(0)
-    for m in (2, 3):
-        for ahead in (True, False):
-            ring_wait(m, 3, ahead)
-    multiply(1, 4, 5)
-    spread_partial(1)
-    total_and_spread(1)
-    for pair in (0, 1):
-        all_of(proj, pair, a_send, a_recv).wait_recv()
+    with jax.named_scope("total_0"):
+        total_and_spread(0)
+    with jax.named_scope("last_wait"):
+        for m in (2, 3):
+            for ahead in (True, False):
+                ring_wait(m, 3, ahead)
+    with jax.named_scope("multiply_1d"):
+        multiply(1, 4, 5)
+    with jax.named_scope("spread_1"):
+        spread_partial(1)
+    with jax.named_scope("total_1"):
+        total_and_spread(1)
+    with jax.named_scope("proj_wait"):
+        for pair in (0, 1):
+            all_of(proj, pair, a_send, a_recv).wait_recv()
 
     side = width // NY
     low = side // 2
@@ -261,20 +281,18 @@
     size = count * tile
     zland[lanes(z, size), :] = own_piece[...]
 
-    def to_z(k, _):
+    for k in Z_STEPS:
         pltpu.make_async_remote_copy(
             src_ref=own_piece, dst_ref=zland.at[lanes(z, size), :],
             send_sem=z_send, recv_sem=z_recv, device_id=z_peer(k), device_id_type=MESH,
         ).start()
-        return 0
-
-    lax.fori_loop(1, NZ, to_z, 0)
     view = zland.at[pl.ds(0, (NZ - 1) * size), :]
     z_all = pltpu.make_async_remote_copy(
         src_ref=view, dst_ref=view, send_sem=z_send, recv_sem=z_recv,
         device_id=z_peer(1), device_id_type=MESH,
     )
-    z_all.wait_recv()
+    with jax.named_scope("z_wait"):
+        z_all.wait_recv()
     total = zland[pl.ds(0, size), :]
     for k in range(1, NZ):
         total = total + zland[pl.ds(k * size, size), :]
@@ -284,39 +302,66 @@
 
     mine = packed_rows(core, y, x, 1)
     packed[mine, :] = total
-    for k in range(1, NX * NY):
-        kx, ky = k % NX, k // NX
-        r2 = ((x + kx) % NX) * 2 + core
-        pltpu.make_async_remote_copy(
-            src_ref=packed.at[mine, :], dst_ref=packed.at[mine, :],
-            send_sem=g_send, recv_sem=g_recv.at[ky],
-            device_id=(r2, ((y + ky) % NY) * NZ + z), device_id_type=MESH,
-        ).start()
-    partner = (x * 2 + 1 - core, c)
-    crossings = []
-    for ky in range(NY):
-        y2 = (y - ky + NY) % NY
-        view = packed.at[pl.ds(0, (NX - 1 if ky == 0 else NX) * size), :]
-        pltpu.make_async_remote_copy(
-            src_ref=view, dst_ref=view, send_sem=g_send, recv_sem=g_recv.at[ky],
-            device_id=partner, device_id_type=MESH,
-        ).wait_recv()
-        at = packed_rows(core, y2, 0, NX)
-        copy = pltpu.make_async_remote_copy(
-            src_ref=packed.at[at, :], dst_ref=packed.at[at, :],
-            send_sem=d_send.at[ky], recv_sem=d_recv.at[ky],
-            device_id=partner, device_id_type=MESH,
-        )
-        copy.start()
-        crossings.append(copy)
-    for ky in range(NY):
-        at = packed_rows(1 - core, (y - ky + NY) % NY, 0, NX)
-        pltpu.make_async_remote_copy(
-            src_ref=packed.at[at, :], dst_ref=packed.at[at, :],
-            send_sem=d_send.at[ky], recv_sem=d_recv.at[ky],
-            device_id=partner, device_id_type=MESH,
-        ).wait_recv()
-
+    for k in range(PLANE - 1):
+        r2, _, c2 = plane_peer(k)
+        if PEERS[k][2] == 0:
+            pltpu.make_async_remote_copy(
+                src_ref=packed.at[mine, :], dst_ref=packed.at[mine, :],
+                send_sem=g_send, recv_sem=g_recv.at[PEERS[k][1]],
+                device_id=(r2, c2), device_id_type=MESH,
+            ).start()
+    with jax.named_scope("gram_gather"):
+        partner = (x * 2 + 1 - core, c)
+        crossings = []
+        for ky in range(NY):
+            y2 = (y - ky + NY) % NY
+            view = packed.at[pl.ds(0, (NX - 1 if ky == 0 else NX) * size), :]
+            pltpu.make_async_remote_copy(
+                src_ref=view, dst_ref=view, send_sem=g_send, recv_sem=g_recv.at[ky],
+                device_id=partner, device_id_type=MESH,
+            ).wait_recv()
+            at = packed_rows(core, y2, 0, NX)
+            copy = pltpu.make_async_remote_copy(
+                src_ref=packed.at[at, :], dst_ref=packed.at[at, :],
+                send_sem=d_send.at[ky], recv_sem=d_recv.at[ky],
+                device_id=partner, device_id_type=MESH,
+            )
+            copy.start()
+            crossings.append(copy)
+        for ky in range(NY):
+            at = packed_rows(1 - core, (y - ky + NY) % NY, 0, NX)
+            pltpu.make_async_remote_copy(
+                src_ref=packed.at[at, :], dst_ref=packed.at[at, :],
+                send_sem=d_send.at[ky], recv_sem=d_recv.at[ky],
+                device_id=partner, device_id_type=MESH,
+            ).wait_recv()
+
+    own_cols[...] = proj[lanes(y, cols), :]
+
+    with jax.named_scope("send_waits"):
+        for copy in copies + crossings:
+            copy.wait_send()
+        for k in range(1, NY):
+            y_copy(k).wait_send()
+        for pair in (0, 1):
+            all_of(land, pair, p_send, p_recv).wait_send()
+            all_of(proj, pair, a_send, a_recv).wait_send()
+        z_all.wait_send()
+        view = zland.at[pl.ds(0, size), :]
+        for k in range(1, NX * NY):
+            pltpu.make_async_remote_copy(
+                src_ref=view, dst_ref=view, send_sem=g_send, recv_sem=g_recv.at[0],
+                device_id=partner, device_id_type=MESH,
+            ).wait_send()
+
+
+def polar_kernel(packed, own_cols, root, right, t, u_hi, u_lo, b_hi, b_lo, v):
+    r, c = lax.axis_index("row"), lax.axis_index("col")
+    width = t.shape[0]
+    cols = own_cols.shape[0]
+    wide_len, col_len = root.shape[1], root.shape[0]
+    side = width // NY
+    low = side // 2
     squares = jnp.zeros((low, side), F32)
     for b in range(10):
         o, i = b // NY, b % NY
@@ -333,53 +378,68 @@
     root_scale = jnp.sqrt(scale)
     t[...] = t[...] / scale
 
-    wide_len, col_len = root.shape[1], root.shape[0]
-    v[pl.ds(0, cols), :] = proj[lanes(y, cols), :]
+    size = width // 2
+    a, b, full = pl.ds(0, size), pl.ds(size, size), pl.ds(0, width)
+    tail = pl.ds(width, cols + col_len)
+    v[pl.ds(0, cols), :] = own_cols[...]
     v[pl.ds(cols, col_len), :] = t[lanes(c, col_len), :]
 
-    def split_t():
-        hi, lo = split(t[...])
-        t_hi[...] = hi
-        t_lo[...] = lo
-
-    def advance():
-        vh, vl = split(v[...])
-        v[...] = 1.5 * v[...] - 0.5 * product(vh, vl, t_hi[...], t_lo[...])
-
-    def step(_, carry):
-        split_t()
-        advance()
-        b = product(t_hi[...], t_lo[...], t_hi[...], t_lo[...])
-        hi, lo = split(b)
-        b_hi[...] = hi
-        b_lo[...] = lo
-        t[...] = (2.25 * t[...] - 1.5 * b) + 0.25 * product(
-            b_hi[...], b_lo[...], t_hi[...], t_lo[...]
-        )
-        return carry
-
-    lax.fori_loop(0, ITERS - 1, step, 0)
-    split_t()
-    advance()
+    def put(slot, rows, at, value):
+        hi, lo = split(value)
+        u_hi[slot, rows, at] = hi
+        u_lo[slot, rows, at] = lo
+
+    def put_b(rows, at, value):
+        hi, lo = split(value)
+        b_hi[rows, at] = hi
+        b_lo[rows, at] = lo
+
+    put(0, full, full, t[...])
+    put(0, tail, full, v[...])
+    for step in range(ITERS):
+        now, new = step % 2, (step + 1) % 2
+
+        def by_t(rows, at):
+            return product(
+                u_hi[now, rows, :], u_lo[now, rows, :], u_hi[now, full, at], u_lo[now, full, at]
+            )
+
+        def by_b(rows, at):
+            return product(u_hi[now, rows, :], u_lo[now, rows, :], b_hi[full, at], b_lo[full, at])
+
+        if step == ITERS - 1:
+            v[...] = 1.5 * v[...] - 0.5 * by_t(tail, full)
+            break
+        value = by_t(a, a)
+        put_b(a, a, value)
+        t[a, a] = 2.25 * t[a, a] - 1.5 * value
+        value = by_t(b, a)
+        put_b(b, a, value)
+        put_b(a, b, value.T)
+        t[b, a] = 2.25 * t[b, a] - 1.5 * value
+        value = by_t(b, b)
+        left, right_half = by_t(tail, a), by_t(tail, b)
+        put_b(b, b, value)
+        t[b, b] = 2.25 * t[b, b] - 1.5 * value
+        first, second = by_b(a, a), by_b(b, a)
+        for at, moved in ((a, left), (b, right_half)):
+            value = 1.5 * v[:, at] - 0.5 * moved
+            v[:, at] = value
+            put(new, tail, at, value)
+        value = t[a, a] + 0.25 * first
+        t[a, a] = value
+        put(new, a, a, value)
+        value = t[b, a] + 0.25 * second
+        t[b, a] = value
+        put(new, b, a, value)
+        put(new, a, b, value.T)
+        value = t[b, b] + 0.25 * by_b(b, b)
+        t[b, b] = value
+        put(new, b, b, value)
     right[...] = v[pl.ds(0, cols), :] / root_scale
     ours = v[pl.ds(cols, col_len), :] * root_scale
     turn = (width - r * wide_len) % width
     root[...] = pltpu.roll(ours, turn, 1)[:, :wide_len]
-
-    for copy in copies + crossings:
-        copy.wait_send()
-    for k in range(1, NY):
-        y_copy(k).wait_send()
-    for pair in (0, 1):
-        all_of(land, pair, p_send, p_recv).wait_send()
-        all_of(proj, pair, a_send, a_recv).wait_send()
-    z_all.wait_send()
-    view = zland.at[pl.ds(0, size), :]
-    for k in range(1, NX * NY):
-        pltpu.make_async_remote_copy(
-            src_ref=view, dst_ref=view, send_sem=g_send, recv_sem=g_recv.at[0],
-            device_id=partner, device_id_type=MESH,
-        ).wait_send()
 
 
 def local(matrix, basis):
@@ -392,11 +452,11 @@
     dma = pltpu.SemaphoreType.DMA
     vmem = pl.BlockSpec(memory_space=pltpu.VMEM)
     hbm = pl.BlockSpec(memory_space=pltpu.HBM)
-    root, right = pl.pallas_call(
-        step_kernel,
-        name="step",
+    packed, own_cols = pl.pallas_call(
+        gather_kernel,
+        name="gather",
         out_shape=(
-            jax.ShapeDtypeStruct((col_len, row_len), F32),
+            jax.ShapeDtypeStruct((PLANE * size, side), F32),
             jax.ShapeDtypeStruct((cols, width), F32),
         ),
         in_specs=[hbm, hbm],
@@ -413,22 +473,34 @@
             pltpu.VMEM((2 * side, side), F32),
             pltpu.VMEM((size, side), F32),
             pltpu.VMEM((NZ * size, side), F32),
-            pltpu.VMEM((PLANE * size, side), F32),
-            pltpu.VMEM((width, width), F32),
-            pltpu.VMEM((width, width), BF16),
-            pltpu.VMEM((width, width), BF16),
-            pltpu.VMEM((width, width), BF16),
-            pltpu.VMEM((width, width), BF16),
-            pltpu.VMEM((cols + col_len, width), F32),
             dma((NY - 1,)), dma((NY - 1,)),
             dma((4, 4)), dma((4, 4)), dma((4, 4)), dma((4, 4)), dma((2,)),
             dma((2,)), dma((2,)), dma((2,)), dma((2,)),
             dma, dma, dma, dma((NY,)), dma((NY,)), dma((NY,)),
         ],
         compiler_params=pltpu.CompilerParams(
-            collective_id=0, has_side_effects=True, vmem_limit_bytes=60 * 2**20
+            collective_id=0, has_side_effects=True, vmem_limit_bytes=48 * 2**20
         ),
-    )(matrix, basis)
+    )(*(pltpu.with_memory_space_constraint(a, pltpu.HBM) for a in (matrix, basis)))
+    root, right = pl.pallas_call(
+        polar_kernel,
+        name="polar",
+        out_shape=(
+            jax.ShapeDtypeStruct((col_len, row_len), F32),
+            jax.ShapeDtypeStruct((cols, width), F32),
+        ),
+        in_specs=[vmem, vmem],
+        out_specs=(vmem, vmem),
+        scratch_shapes=[
+            pltpu.VMEM((width, width), F32),
+            pltpu.VMEM((2, width + cols + col_len, width), BF16),
+            pltpu.VMEM((2, width + cols + col_len, width), BF16),
+            pltpu.VMEM((width, width), BF16),
+            pltpu.VMEM((width, width), BF16),
+            pltpu.VMEM((cols + col_len, width), F32),
+        ],
+        compiler_params=pltpu.CompilerParams(vmem_limit_bytes=24 * 2**20),
+    )(packed, own_cols)
     return root.T, right
 
 

time: 104 us -> 93.6 us (0.90)
  Pallas kernels: 101 us -> 92.9 us
  local copies, waits for them, and re-layouts: 2.86 us -> 0 us
    pallas_call x1 -> x2, Pallas kernels: 101 us -> 92.9 us  [the longest x1 80.6 us: local(): pl.pallas_call(gather_kernel, name='gather', out_shape=(jax.ShapeDtypeStr...]
    unnamed x2 -> x0, local copies, waits for them, and re-layouts: 2.86 us -> none
where the time goes in v3:
time: 93.6 us; the launch traced here: 93.5 us
  Pallas kernels  92.9 us (99%)
    pallas_call x1, Pallas kernels, local(): pl.pallas_call(gather_kernel, name='gather', out_shape=(jax.ShapeDtypeStr...  80.6 us
    pallas_call x1, Pallas kernels, local(): pl.pallas_call(polar_kernel, name='polar', out_shape=(jax.ShapeDtypeStruc...  12.3 us

profile of v3, /device:TPU:1, one launch (start us, length us, event | category | flops | bytes accessed | tf_op | source)
XLA Modules:
  0.0 93.5 jit_solution(11322873884401724259)
XLA Ops:
  0.6 80.6 %gather.1 = (f32[1280,128]{1,0:T(8,128)S(1)}, f32[64,512]{1,0:T(8,128)S(1)}) custom-call(f32[64,8192]{1,0:T(8,128)} %mat_hbm.1, f32[256,512]{1,0:T(8,128)} %bas_hbm.1), custom_call_target="tpu_custom_call" | custom-call | tf_op jit(solution)/shard_map/gather/pallas_call | solution.py:455
  81.2 12.3 %polar.1 = (f32[16,64]{1,0:T(8,128)}, f32[64,512]{1,0:T(8,128)}) custom-call(f32[1280,128]{1,0:T(8,128)S(1)} %get-tuple-element.6.packed, f32[64,512]{1,0:T(8,128)S(1)} %get-tuple-element.7.own_cols), custom_call_target="tpu_custom_call" | custom-call | tf_op jit(solution)/shard_map/polar/pallas_call | solution.py:485

commit v4 on v3

--- a/solution.py
+++ b/solution.py
@@ -42,7 +42,7 @@
     mat_hbm, bas_hbm, packed, own_cols,
     mat, m_in, m_hi, m_lo, q, acc, land, proj, block, own_piece, zland,
     y_send, y_recv, f_send, f_recv, b_send, b_recv, local_sem,
-    p_send, p_recv, a_send, a_recv, z_send, z_recv, g_send, g_recv, d_send, d_recv,
+    p_send, p_recv, a_send, a_recv, z_send, z_recv, g_send, g_recv, d_send, d_recv, plane_sem,
 ):
     r, c = lax.axis_index("row"), lax.axis_index("col")
     y, z = c // NZ, c % NZ
@@ -73,13 +73,16 @@
 
     barrier = pltpu.get_barrier_semaphore()
 
-    for k in Z_STEPS:
-        pl.semaphore_signal(barrier, inc=1, device_id=z_peer(k), device_id_type=MESH)
+    near = [z_peer(1), z_peer(NZ - 1)] + [(r, near_col[d]) for d in range(1, NY)]
     for k in range(PLANE - 1):
-        r2, _, c2 = plane_peer(k)
-        pl.semaphore_signal(barrier, inc=1, device_id=(r2, c2), device_id_type=MESH)
+        if PEERS[k][1] == 0:
+            near.append((plane_peer(k)[0], c))
+    for peer in near:
+        pl.semaphore_signal(barrier, inc=1, device_id=peer, device_id_type=MESH)
     with jax.named_scope("barrier"):
-        pl.semaphore_wait(barrier, PLANE - 1 + NZ - 1)
+        pl.semaphore_wait(barrier, len(near))
+    for d in range(1, NY):
+        pl.semaphore_signal(plane_sem, inc=1, device_id=(r, near_col[d]), device_id_type=MESH)
 
     def ring_copy(m, d, ahead):
         sign = 1 if ahead else -1
@@ -153,8 +156,10 @@
         m_lo[at, :] = lo
         return 0
 
-    def multiply(pair, first, last):
-        here = pl.ds(pair * 2 * wide, 2 * wide)
+    groups = [pl.ds(0, 2 * wide), pl.ds(2 * wide, wide), pl.ds(3 * wide, wide)]
+    late = pl.ds(2 * wide, 2 * wide)
+
+    def multiply(here, first, last):
 
         def one(o, _):
             owner = (z + o) % NZ
@@ -165,31 +170,30 @@
 
         lax.fori_loop(first, last, one, 0)
 
-    def spread_partial(pair):
-        here = pl.ds(pair * 2 * wide, 2 * wide)
+    def spread_partial(group):
+        here = groups[group]
 
         for k in range(PLANE - 1):
             r2, y2, c2 = plane_peer(k)
             src = pl.ds(pl.multiple_of(y2 * cols + r2 * piece, piece), piece)
             pltpu.make_async_remote_copy(
                 src_ref=acc.at[src, here], dst_ref=land.at[pl.ds(k * piece, piece), here],
-                send_sem=p_send.at[pair], recv_sem=p_recv.at[pair],
+                send_sem=p_send.at[group], recv_sem=p_recv.at[group],
                 device_id=(r2, c2), device_id_type=MESH,
             ).start()
 
     mine = pl.ds(pl.multiple_of(y * cols + r * piece, piece), piece)
 
-    def all_of(ref, pair, send, recv):
-        here = pl.ds(pair * 2 * wide, 2 * wide)
-        view = ref.at[pl.ds(0, (PLANE - 1) * piece), here]
+    def all_of(ref, group, send, recv):
+        view = ref.at[pl.ds(0, (PLANE - 1) * piece), groups[group]]
         return pltpu.make_async_remote_copy(
-            src_ref=view, dst_ref=view, send_sem=send.at[pair], recv_sem=recv.at[pair],
+            src_ref=view, dst_ref=view, send_sem=send.at[group], recv_sem=recv.at[group],
             device_id=z_peer(1), device_id_type=MESH,
         )
 
-    def total_and_spread(pair):
-        here = pl.ds(pair * 2 * wide, 2 * wide)
-        all_of(land, pair, p_send, p_recv).wait_recv()
+    def total_and_spread(group):
+        here = groups[group]
+        all_of(land, group, p_send, p_recv).wait_recv()
         total = acc[mine, here]
         for k in range(PLANE - 1):
             total = total + land[pl.ds(k * piece, piece), here]
@@ -199,7 +203,7 @@
             r2, _, c2 = plane_peer(k)
             pltpu.make_async_remote_copy(
                 src_ref=proj.at[mine, here], dst_ref=proj.at[mine, here],
-                send_sem=a_send.at[pair], recv_sem=a_recv.at[pair],
+                send_sem=a_send.at[group], recv_sem=a_recv.at[group],
                 device_id=(r2, c2), device_id_type=MESH,
             ).start()
 
@@ -230,8 +234,9 @@
         for ahead in (True, False):
             ring_wait(m, 3, ahead)
     with jax.named_scope("multiply_0"):
-        multiply(0, 0, NZ)
+        multiply(groups[0], 0, NZ)
     with jax.named_scope("spread_0"):
+        pl.semaphore_wait(plane_sem, NY - 1)
         spread_partial(0)
     with jax.named_scope("issue_31"):
         issue(3, 1)
@@ -239,28 +244,30 @@
         issue(2, 2)
     with jax.named_scope("issue_32"):
         issue(3, 2)
-    multiply(1, 0, 3)
+    multiply(late, 0, 3)
     with jax.named_scope("issue_23"):
         issue(2, 3)
     with jax.named_scope("issue_33"):
         issue(3, 3)
-    multiply(1, 3, 4)
-    multiply(1, 5, NZ)
+    multiply(late, 3, 4)
+    multiply(late, 5, NZ)
     with jax.named_scope("total_0"):
         total_and_spread(0)
-    with jax.named_scope("last_wait"):
-        for m in (2, 3):
+    for m in (2, 3):
+        with jax.named_scope("last_wait"):
             for ahead in (True, False):
                 ring_wait(m, 3, ahead)
-    with jax.named_scope("multiply_1d"):
-        multiply(1, 4, 5)
-    with jax.named_scope("spread_1"):
-        spread_partial(1)
+        with jax.named_scope("multiply_last"):
+            multiply(groups[m - 1], 4, 5)
+        with jax.named_scope("spread_last"):
+            spread_partial(m - 1)
     with jax.named_scope("total_1"):
         total_and_spread(1)
+    with jax.named_scope("total_2"):
+        total_and_spread(2)
     with jax.named_scope("proj_wait"):
-        for pair in (0, 1):
-            all_of(proj, pair, a_send, a_recv).wait_recv()
+        for group in range(3):
+            all_of(proj, group, a_send, a_recv).wait_recv()
 
     side = width // NY
     low = side // 2
@@ -343,9 +350,9 @@
             copy.wait_send()
         for k in range(1, NY):
             y_copy(k).wait_send()
-        for pair in (0, 1):
-            all_of(land, pair, p_send, p_recv).wait_send()
-            all_of(proj, pair, a_send, a_recv).wait_send()
+        for group in range(3):
+            all_of(land, group, p_send, p_recv).wait_send()
+            all_of(proj, group, a_send, a_recv).wait_send()
         z_all.wait_send()
         view = zland.at[pl.ds(0, size), :]
         for k in range(1, NX * NY):
@@ -396,7 +403,7 @@
 
     put(0, full, full, t[...])
     put(0, tail, full, v[...])
-    for step in range(ITERS):
+    for step in range(ITERS - 1):
         now, new = step % 2, (step + 1) % 2
 
         def by_t(rows, at):
@@ -407,8 +414,20 @@
         def by_b(rows, at):
             return product(u_hi[now, rows, :], u_lo[now, rows, :], b_hi[full, at], b_lo[full, at])
 
-        if step == ITERS - 1:
-            v[...] = 1.5 * v[...] - 0.5 * by_t(tail, full)
+        if step == ITERS - 2:
+            def times_t(value):
+                hi, lo = split(value)
+                both = jnp.concatenate([hi, lo], axis=0)
+                dot = functools.partial(jnp.dot, preferred_element_type=F32)
+                wide = dot(both, u_hi[now, full, :])
+                rows = value.shape[0]
+                return (wide[:rows] + wide[rows:]) + dot(hi, u_lo[now, full, :])
+
+            def times_s(value):
+                return 1.5 * value - 0.5 * times_t(value)
+
+            value = times_s(v[...])
+            v[...] = 1.5 * value - 0.5 * times_s(times_s(times_t(value)))
             break
         value = by_t(a, a)
         put_b(a, a, value)
@@ -475,8 +494,9 @@
             pltpu.VMEM((NZ * size, side), F32),
             dma((NY - 1,)), dma((NY - 1,)),
             dma((4, 4)), dma((4, 4)), dma((4, 4)), dma((4, 4)), dma((2,)),
-            dma((2,)), dma((2,)), dma((2,)), dma((2,)),
+            dma((3,)), dma((3,)), dma((3,)), dma((3,)),
             dma, dma, dma, dma((NY,)), dma((NY,)), dma((NY,)),
+            pltpu.SemaphoreType.REGULAR,
         ],
         compiler_params=pltpu.CompilerParams(
             collective_id=0, has_side_effects=True, vmem_limit_bytes=48 * 2**20

time: 93.6 us -> 91.4 us (0.976)
  Pallas kernels: 92.9 us -> 90.7 us
    pallas_call x1, Pallas kernels: 80.6 us -> 79 us  [local(): pl.pallas_call(gather_kernel, name='gather', out_shape=(jax.ShapeDtypeStr...]
where the time goes in v4:
time: 91.4 us; the launch traced here: 91.3 us
  Pallas kernels  90.7 us (99%)
    pallas_call x1, Pallas kernels, local(): pl.pallas_call(gather_kernel, name='gather', out_shape=(jax.ShapeDtypeStr...  79 us
    pallas_call x1, Pallas kernels, local(): pl.pallas_call(polar_kernel, name='polar', out_shape=(jax.ShapeDtypeStruc...  11.7 us

profile of v4, /device:TPU:1, one launch (start us, length us, event | category | flops | bytes accessed | tf_op | source)
XLA Modules:
  0.0 91.3 jit_solution(16936533624392594073)
XLA Ops:
  0.6 79.0 %gather.1 = (f32[1280,128]{1,0:T(8,128)S(1)}, f32[64,512]{1,0:T(8,128)S(1)}) custom-call(f32[64,8192]{1,0:T(8,128)} %mat_hbm.1, f32[256,512]{1,0:T(8,128)} %bas_hbm.1), custom_call_target="tpu_custom_call" | custom-call | tf_op jit(solution)/shard_map/gather/pallas_call | solution.py:474
  79.6 11.7 %polar.1 = (f32[16,64]{1,0:T(8,128)}, f32[64,512]{1,0:T(8,128)}) custom-call(f32[1280,128]{1,0:T(8,128)S(1)} %get-tuple-element.6.packed, f32[64,512]{1,0:T(8,128)S(1)} %get-tuple-element.7.own_cols), custom_call_target="tpu_custom_call" | custom-call | tf_op jit(solution)/shard_map/polar/pallas_call | solution.py:505

commit v5 on v4

--- a/solution.py
+++ b/solution.py
@@ -39,8 +39,9 @@
 
 
 def gather_kernel(
-    mat_hbm, bas_hbm, packed, own_cols,
-    mat, m_in, m_hi, m_lo, q, acc, land, proj, block, own_piece, zland,
+    mat_hbm, bas_hbm, packed_early, packed_late, own_cols,
+    mat, m_in, m_hi, m_lo, q, acc, land, proj, block,
+    piece_early, piece_late, zland_early, zland_late,
     y_send, y_recv, f_send, f_recv, b_send, b_recv, local_sem,
     p_send, p_recv, a_send, a_recv, z_send, z_recv, g_send, g_recv, d_send, d_recv, plane_sem,
 ):
@@ -265,104 +266,135 @@
         total_and_spread(1)
     with jax.named_scope("total_2"):
         total_and_spread(2)
-    with jax.named_scope("proj_wait"):
-        for group in range(3):
-            all_of(proj, group, a_send, a_recv).wait_recv()
-
     side = width // NY
     low = side // 2
     tile = 8
     s = y * NX + x
-    count = 10 * low // tile // (NX * NY)
-    first = s * count // (low // tile)
-    for n in range(2):
-        b = (first + n) % 10
-        i = b % NY
-        lh, ll = split(proj[:, lanes(i, side)].T)
-        rh, rl = split(proj[:, lanes((i + b // NY) % NY, side)])
-        block[pl.ds(n * side, side), :] = product(lh, ll, rh, rl)
-    for n in range(count):
-        at = s * count + n
-        row = (at // (low // tile) - first) * side + core * low + at % (low // tile) * tile
-        own_piece[pl.ds(n * tile, tile), :] = block[pl.ds(pl.multiple_of(row, tile), tile), :]
-    size = count * tile
-    zland[lanes(z, size), :] = own_piece[...]
-
-    for k in Z_STEPS:
-        pltpu.make_async_remote_copy(
-            src_ref=own_piece, dst_ref=zland.at[lanes(z, size), :],
-            send_sem=z_send, recv_sem=z_recv, device_id=z_peer(k), device_id_type=MESH,
-        ).start()
-    view = zland.at[pl.ds(0, (NZ - 1) * size), :]
-    z_all = pltpu.make_async_remote_copy(
-        src_ref=view, dst_ref=view, send_sem=z_send, recv_sem=z_recv,
-        device_id=z_peer(1), device_id_type=MESH,
+    partner = (x * 2 + 1 - core, c)
+    rounds = (
+        (6, piece_early, zland_early, packed_early),
+        (4, piece_late, zland_late, packed_late),
     )
-    with jax.named_scope("z_wait"):
-        z_all.wait_recv()
-    total = zland[pl.ds(0, size), :]
-    for k in range(1, NZ):
-        total = total + zland[pl.ds(k * size, size), :]
-
-    def packed_rows(of_core, of_y, of_x, chips):
+
+    def gram_part(turn):
+        blocks, part_of, _, _ = rounds[turn]
+        count = blocks // 2
+        first = s * count // (low // tile)
+        for n in range(2):
+            b = (first + n) % blocks
+            i, j = (b % 3, (b % 3 + b // 3) % 3) if turn == 0 else (b, 3)
+            lh, ll = split(proj[:, lanes(i, side)].T)
+            rh, rl = split(proj[:, lanes(j, side)])
+            block[pl.ds(n * side, side), :] = product(lh, ll, rh, rl)
+        for n in range(count):
+            at = s * count + n
+            row = (at // (low // tile) - first) * side + core * low + at % (low // tile) * tile
+            part_of[pl.ds(n * tile, tile), :] = block[pl.ds(pl.multiple_of(row, tile), tile), :]
+
+    def z_all(turn):
+        _, part_of, landing, _ = rounds[turn]
+        view = landing.at[pl.ds(0, (NZ - 1) * part_of.shape[0]), :]
+        return pltpu.make_async_remote_copy(
+            src_ref=view, dst_ref=view, send_sem=z_send.at[turn], recv_sem=z_recv.at[turn],
+            device_id=z_peer(1), device_id_type=MESH,
+        )
+
+    def spread_z(turn):
+        _, part_of, landing, _ = rounds[turn]
+        own = lanes(z, part_of.shape[0])
+        for k in Z_STEPS:
+            pltpu.make_async_remote_copy(
+                src_ref=part_of, dst_ref=landing.at[own, :],
+                send_sem=z_send.at[turn], recv_sem=z_recv.at[turn],
+                device_id=z_peer(k), device_id_type=MESH,
+            ).start()
+        landing[own, :] = part_of[...]
+
+    def packed_rows(turn, of_core, of_y, of_x, chips):
+        size = rounds[turn][1].shape[0]
         return pl.ds(pl.multiple_of(((of_core * NY + of_y) * NX + of_x) * size, size), chips * size)
 
-    mine = packed_rows(core, y, x, 1)
-    packed[mine, :] = total
-    for k in range(PLANE - 1):
-        r2, _, c2 = plane_peer(k)
-        if PEERS[k][2] == 0:
+    def spread_gram(turn):
+        _, part_of, landing, packed = rounds[turn]
+        size = part_of.shape[0]
+        z_all(turn).wait_recv()
+        total = landing[pl.ds(0, size), :]
+        for k in range(1, NZ):
+            total = total + landing[pl.ds(k * size, size), :]
+        own = packed_rows(turn, core, y, x, 1)
+        packed[own, :] = total
+        for k in range(PLANE - 1):
+            r2, _, c2 = plane_peer(k)
+            if PEERS[k][2] == 0:
+                pltpu.make_async_remote_copy(
+                    src_ref=packed.at[own, :], dst_ref=packed.at[own, :],
+                    send_sem=g_send.at[turn], recv_sem=g_recv.at[turn, PEERS[k][1]],
+                    device_id=(r2, c2), device_id_type=MESH,
+                ).start()
+
+    def crossing(turn, of_core, ky):
+        packed = rounds[turn][3]
+        at = packed_rows(turn, of_core, (y - ky + NY) % NY, 0, NX)
+        return pltpu.make_async_remote_copy(
+            src_ref=packed.at[at, :], dst_ref=packed.at[at, :],
+            send_sem=d_send.at[turn, ky], recv_sem=d_recv.at[turn, ky],
+            device_id=partner, device_id_type=MESH,
+        )
+
+    def cross(turn):
+        _, part_of, _, packed = rounds[turn]
+        for ky in (0, 1, 3, 2):
+            view = packed.at[pl.ds(0, (NX - 1 if ky == 0 else NX) * part_of.shape[0]), :]
             pltpu.make_async_remote_copy(
-                src_ref=packed.at[mine, :], dst_ref=packed.at[mine, :],
-                send_sem=g_send, recv_sem=g_recv.at[PEERS[k][1]],
-                device_id=(r2, c2), device_id_type=MESH,
-            ).start()
-    with jax.named_scope("gram_gather"):
-        partner = (x * 2 + 1 - core, c)
-        crossings = []
-        for ky in range(NY):
-            y2 = (y - ky + NY) % NY
-            view = packed.at[pl.ds(0, (NX - 1 if ky == 0 else NX) * size), :]
-            pltpu.make_async_remote_copy(
-                src_ref=view, dst_ref=view, send_sem=g_send, recv_sem=g_recv.at[ky],
+                src_ref=view, dst_ref=view, send_sem=g_send.at[turn], recv_sem=g_recv.at[turn, ky],
                 device_id=partner, device_id_type=MESH,
             ).wait_recv()
-            at = packed_rows(core, y2, 0, NX)
-            copy = pltpu.make_async_remote_copy(
-                src_ref=packed.at[at, :], dst_ref=packed.at[at, :],
-                send_sem=d_send.at[ky], recv_sem=d_recv.at[ky],
-                device_id=partner, device_id_type=MESH,
-            )
-            copy.start()
-            crossings.append(copy)
-        for ky in range(NY):
-            at = packed_rows(1 - core, (y - ky + NY) % NY, 0, NX)
-            pltpu.make_async_remote_copy(
-                src_ref=packed.at[at, :], dst_ref=packed.at[at, :],
-                send_sem=d_send.at[ky], recv_sem=d_recv.at[ky],
-                device_id=partner, device_id_type=MESH,
-            ).wait_recv()
-
+            crossing(turn, core, ky).start()
+
+    with jax.named_scope("proj_wait"):
+        for group in range(2):
+            all_of(proj, group, a_send, a_recv).wait_recv()
+    gram_part(0)
+    spread_z(0)
+    with jax.named_scope("proj_wait_late"):
+        all_of(proj, 2, a_send, a_recv).wait_recv()
+    gram_part(1)
+    spread_z(1)
+    with jax.named_scope("z_wait"):
+        spread_gram(0)
+    with jax.named_scope("z_wait_late"):
+        spread_gram(1)
+    with jax.named_scope("cross"):
+        cross(0)
+    with jax.named_scope("cross_late"):
+        cross(1)
+    with jax.named_scope("partner_wait"):
+        for turn in range(2):
+            for ky in range(NY):
+                crossing(turn, 1 - core, ky).wait_recv()
     own_cols[...] = proj[lanes(y, cols), :]
 
     with jax.named_scope("send_waits"):
-        for copy in copies + crossings:
+        for copy in copies:
             copy.wait_send()
         for k in range(1, NY):
             y_copy(k).wait_send()
         for group in range(3):
             all_of(land, group, p_send, p_recv).wait_send()
             all_of(proj, group, a_send, a_recv).wait_send()
-        z_all.wait_send()
-        view = zland.at[pl.ds(0, size), :]
-        for k in range(1, NX * NY):
+        for turn in range(2):
+            _, part_of, _, packed = rounds[turn]
+            z_all(turn).wait_send()
+            view = packed.at[pl.ds(0, (NX * NY - 1) * part_of.shape[0]), :]
             pltpu.make_async_remote_copy(
-                src_ref=view, dst_ref=view, send_sem=g_send, recv_sem=g_recv.at[0],
+                src_ref=view, dst_ref=view, send_sem=g_send.at[turn], recv_sem=g_recv.at[turn, 0],
                 device_id=partner, device_id_type=MESH,
             ).wait_send()
-
-
-def polar_kernel(packed, own_cols, root, right, t, u_hi, u_lo, b_hi, b_lo, v):
+            for ky in range(NY):
+                crossing(turn, core, ky).wait_send()
+
+
+def polar_kernel(packed_early, packed_late, own_cols, root, right, t, u_hi, u_lo, b_hi, b_lo, v):
     r, c = lax.axis_index("row"), lax.axis_index("col")
     width = t.shape[0]
     cols = own_cols.shape[0]
@@ -370,24 +402,25 @@
     side = width // NY
     low = side // 2
     squares = jnp.zeros((low, side), F32)
-    for b in range(10):
-        o, i = b // NY, b % NY
-        j = (i + o) % NY
-        for h in range(2):
-            part_of = packed[pl.ds((h * 10 + b) * low, low), :]
-            squares = squares + (1.0 if o == 0 else 2.0) * (part_of * part_of)
-            t[pl.ds(i * side + h * low, low), pl.ds(j * side, side)] = part_of
-        if o:
-            t[pl.ds(j * side, side), pl.ds(i * side, side)] = t[
-                pl.ds(i * side, side), pl.ds(j * side, side)
-            ].T
+    early = [(i, (i + o) % 3) for o in range(2) for i in range(3)]
+    for packed, blocks in ((packed_early, early), (packed_late, [(i, 3) for i in range(4)])):
+        for b, (i, j) in enumerate(blocks):
+            for h in range(2):
+                part_of = packed[pl.ds((h * len(blocks) + b) * low, low), :]
+                squares = squares + (1.0 if i == j else 2.0) * (part_of * part_of)
+                t[pl.ds(i * side + h * low, low), pl.ds(j * side, side)] = part_of
+            if i != j:
+                t[pl.ds(j * side, side), pl.ds(i * side, side)] = t[
+                    pl.ds(i * side, side), pl.ds(j * side, side)
+                ].T
     scale = jnp.sqrt(jnp.full((1, 1), jnp.sum(squares), F32) + 1e-06)
     root_scale = jnp.sqrt(scale)
-    t[...] = t[...] / scale
+    t[...] = t[...] * (1.0 / scale)
 
     size = width // 2
     a, b, full = pl.ds(0, size), pl.ds(size, size), pl.ds(0, width)
     tail = pl.ds(width, cols + col_len)
+    b_tail = pl.ds(size, size + cols + col_len)
     v[pl.ds(0, cols), :] = own_cols[...]
     v[pl.ds(cols, col_len), :] = t[lanes(c, col_len), :]
 
@@ -400,6 +433,9 @@
         hi, lo = split(value)
         b_hi[rows, at] = hi
         b_lo[rows, at] = lo
+
+    def cut(value):
+        return value[:size], value[size:]
 
     put(0, full, full, t[...])
     put(0, tail, full, v[...])
@@ -432,19 +468,14 @@
         value = by_t(a, a)
         put_b(a, a, value)
         t[a, a] = 2.25 * t[a, a] - 1.5 * value
-        value = by_t(b, a)
+        value, left = cut(by_t(b_tail, a))
         put_b(b, a, value)
         put_b(a, b, value.T)
         t[b, a] = 2.25 * t[b, a] - 1.5 * value
-        value = by_t(b, b)
-        left, right_half = by_t(tail, a), by_t(tail, b)
+        value, right_half = cut(by_t(b_tail, b))
         put_b(b, b, value)
         t[b, b] = 2.25 * t[b, b] - 1.5 * value
-        first, second = by_b(a, a), by_b(b, a)
-        for at, moved in ((a, left), (b, right_half)):
-            value = 1.5 * v[:, at] - 0.5 * moved
-            v[:, at] = value
-            put(new, tail, at, value)
+        first, second = cut(by_b(full, a))
         value = t[a, a] + 0.25 * first
         t[a, a] = value
         put(new, a, a, value)
@@ -452,10 +483,15 @@
         t[b, a] = value
         put(new, b, a, value)
         put(new, a, b, value.T)
-        value = t[b, b] + 0.25 * by_b(b, b)
+        last = by_b(b, b)
+        for at, moved in ((a, left), (b, right_half)):
+            value = 1.5 * v[:, at] - 0.5 * moved
+            v[:, at] = value
+            put(new, tail, at, value)
+        value = t[b, b] + 0.25 * last
         t[b, b] = value
         put(new, b, b, value)
-    right[...] = v[pl.ds(0, cols), :] / root_scale
+    right[...] = v[pl.ds(0, cols), :] * (1.0 / root_scale)
     ours = v[pl.ds(cols, col_len), :] * root_scale
     turn = (width - r * wide_len) % width
     root[...] = pltpu.roll(ours, turn, 1)[:, :wide_len]
@@ -466,20 +502,21 @@
     rows, width = basis.shape
     part = depth // NY
     side = width // NY
-    size = 10 * side // (2 * NX * NY)
+    early, late = 6 * side // (2 * NX * NY), 4 * side // (2 * NX * NY)
     row_len, col_len = width // NR, width // (NY * NZ)
     dma = pltpu.SemaphoreType.DMA
     vmem = pl.BlockSpec(memory_space=pltpu.VMEM)
     hbm = pl.BlockSpec(memory_space=pltpu.HBM)
-    packed, own_cols = pl.pallas_call(
+    packed_early, packed_late, own_cols = pl.pallas_call(
         gather_kernel,
         name="gather",
         out_shape=(
-            jax.ShapeDtypeStruct((PLANE * size, side), F32),
+            jax.ShapeDtypeStruct((PLANE * early, side), F32),
+            jax.ShapeDtypeStruct((PLANE * late, side), F32),
             jax.ShapeDtypeStruct((cols, width), F32),
         ),
         in_specs=[hbm, hbm],
-        out_specs=(vmem, vmem),
+        out_specs=(vmem, vmem, vmem),
         scratch_shapes=[
             pltpu.VMEM((cols, depth), F32),
             pltpu.VMEM((NY * cols, part), F32),
@@ -490,12 +527,14 @@
             pltpu.VMEM(((PLANE - 1) * cols // NR, width), F32),
             pltpu.VMEM((NY * cols, width), F32),
             pltpu.VMEM((2 * side, side), F32),
-            pltpu.VMEM((size, side), F32),
-            pltpu.VMEM((NZ * size, side), F32),
+            pltpu.VMEM((early, side), F32),
+            pltpu.VMEM((late, side), F32),
+            pltpu.VMEM((NZ * early, side), F32),
+            pltpu.VMEM((NZ * late, side), F32),
             dma((NY - 1,)), dma((NY - 1,)),
             dma((4, 4)), dma((4, 4)), dma((4, 4)), dma((4, 4)), dma((2,)),
             dma((3,)), dma((3,)), dma((3,)), dma((3,)),
-            dma, dma, dma, dma((NY,)), dma((NY,)), dma((NY,)),
+            dma((2,)), dma((2,)), dma((2,)), dma((2, NY)), dma((2, NY)), dma((2, NY)),
             pltpu.SemaphoreType.REGULAR,
         ],
         compiler_params=pltpu.CompilerParams(
@@ -509,7 +548,7 @@
             jax.ShapeDtypeStruct((col_len, row_len), F32),
             jax.ShapeDtypeStruct((cols, width), F32),
         ),
-        in_specs=[vmem, vmem],
+        in_specs=[vmem, vmem, vmem],
         out_specs=(vmem, vmem),
         scratch_shapes=[
             pltpu.VMEM((width, width), F32),
@@ -520,7 +559,7 @@
             pltpu.VMEM((cols + col_len, width), F32),
         ],
         compiler_params=pltpu.CompilerParams(vmem_limit_bytes=24 * 2**20),
-    )(packed, own_cols)
+    )(packed_early, packed_late, own_cols)
     return root.T, right
 
 

time: 91.4 us -> 88.4 us (0.967)
  Pallas kernels: 90.7 us -> 87.6 us
    pallas_call x1, Pallas kernels: 79 us -> 76.7 us  [local(): pl.pallas_call(gather_kernel, name='gather', out_shape=(jax.ShapeDtypeStr...]
where the time goes in v5:
time: 88.4 us; the launch traced here: 88.2 us
  Pallas kernels  87.6 us (99%)
    pallas_call x1, Pallas kernels, local(): pl.pallas_call(gather_kernel, name='gather', out_shape=(jax.ShapeDtypeStr...  76.7 us
    pallas_call x1, Pallas kernels, local(): pl.pallas_call(polar_kernel, name='polar', out_shape=(jax.ShapeDtypeStruc...  10.9 us

profile of v5, /device:TPU:1, one launch (start us, length us, event | category | flops | bytes accessed | tf_op | source)
XLA Modules:
  0.0 88.2 jit_solution(434475134213695437)
XLA Ops:
  0.6 76.7 %gather.1 = (f32[768,128]{1,0:T(8,128)S(1)}, f32[512,128]{1,0:T(8,128)S(1)}, f32[64,512]{1,0:T(8,128)S(1)}) custom-call(f32[64,8192]{1,0:T(8,128)} %mat_hbm.1, f32[256,512]{1,0:T(8,128)} %bas_hbm.1), custom_call_target="tpu_custom_call" | custom-call | tf_op jit(solution)/shard_map/gather/pallas_call | solution.py:510
  77.4 10.9 %polar.1 = (f32[16,64]{1,0:T(8,128)}, f32[64,512]{1,0:T(8,128)}) custom-call(f32[768,128]{1,0:T(8,128)S(1)} %get-tuple-element.7.packed_early, f32[512,128]{1,0:T(8,128)S(1)} %get-tuple-element.8.packed_late, f32[64,512]{1,0:T(8,128)S(1)} %get-tuple-element.9.own_cols), custom_call_target="tpu_custom_call" | custom-call | tf_op jit(solution)/shard_map/polar/pallas_call | solution.py:544

commit v6 on v5

--- a/solution.py
+++ b/solution.py
@@ -85,34 +85,23 @@
     for d in range(1, NY):
         pl.semaphore_signal(plane_sem, inc=1, device_id=(r, near_col[d]), device_id_type=MESH)
 
-    def ring_copy(m, d, ahead):
-        sign = 1 if ahead else -1
-        owner = (z - sign * d + NZ) % NZ
-        here = pl.ds(m * wide, wide)
+    def ring_item(m, d, part, ahead, behind):
+        owner = (z - (behind if ahead else -behind) + NZ) % NZ
         span = pl.ds(pl.multiple_of(owner * rows, rows), rows)
-        if d == 3:
-            start = owner * rows + (0 if ahead else half)
+        if part is not None:
+            start = owner * rows + (0 if ahead == (part == 0) else half)
             span = pl.ds(pl.multiple_of(start, half), half)
+        view = q.at[span, pl.ds(m * wide, wide)]
         send, recv = (f_send, f_recv) if ahead else (b_send, b_recv)
+        at = d + 3 * (part or 0)
         return pltpu.make_async_remote_copy(
-            src_ref=q.at[span, here], dst_ref=q.at[span, here], send_sem=send.at[m, d], recv_sem=recv.at[m, d],
-            device_id=(r, y * NZ + (z + sign + NZ) % NZ), device_id_type=MESH,
+            src_ref=view, dst_ref=view, send_sem=send.at[m, at], recv_sem=recv.at[m, at],
+            device_id=(r, y * NZ + (z + (1 if ahead else -1) + NZ) % NZ), device_id_type=MESH,
         )
 
-    def ring_wait(m, d, ahead):
-        sign = 1 if ahead else -1
-        owner = (z - sign * (d + 1) + NZ) % NZ
-        here = pl.ds(m * wide, wide)
-        span = pl.ds(pl.multiple_of(owner * rows, rows), rows)
-        if d == 3:
-            start = owner * rows + (0 if ahead else half)
-            span = pl.ds(pl.multiple_of(start, half), half)
-        send, recv = (f_send, f_recv) if ahead else (b_send, b_recv)
-        pltpu.make_async_remote_copy(
-            src_ref=q.at[span, here], dst_ref=q.at[span, here],
-            send_sem=send.at[m, d], recv_sem=recv.at[m, d],
-            device_id=(r, y * NZ + (z + sign + NZ) % NZ), device_id_type=MESH,
-        ).wait_recv()
+    def ring_wait(m, d, part=None):
+        for ahead in (True, False):
+            ring_item(m, d, part, ahead, d + 1).wait_recv()
 
     def y_copy(k):
         y2 = (y + k) % NY
@@ -132,11 +121,9 @@
 
     copies = []
 
-    def issue(m, d):
+    def issue(m, d, part=None):
         for ahead in (True, False):
-            if d > 0:
-                ring_wait(m, d - 1, ahead)
-            copy = ring_copy(m, d, ahead)
+            copy = ring_item(m, d, part, ahead, d)
             copy.start()
             copies.append(copy)
 
@@ -158,7 +145,6 @@
         return 0
 
     groups = [pl.ds(0, 2 * wide), pl.ds(2 * wide, wide), pl.ds(3 * wide, wide)]
-    late = pl.ds(2 * wide, 2 * wide)
 
     def multiply(here, first, last):
 
@@ -216,56 +202,77 @@
     issue(1, 0)
     acc[...] = jnp.zeros_like(acc)
     lax.fori_loop(0, cols // 16, own_split, 0)
-    for d in range(1, 4):
-        with jax.named_scope(f"issue_0{d}"):
-            issue(0, d)
-        with jax.named_scope(f"issue_1{d}"):
-            issue(1, d)
-    with jax.named_scope("issue_20"):
-        issue(2, 0)
-    with jax.named_scope("issue_30"):
-        issue(3, 0)
+    for m, d in ((0, 1), (1, 1), (0, 2), (1, 2)):
+        with jax.named_scope(f"issue_{m}{d}"):
+            ring_wait(m, d - 1)
+            issue(m, d)
+    issue(2, 0)
+    issue(3, 0)
     with jax.named_scope("issue_21"):
+        for m in (0, 1):
+            ring_wait(m, 2)
+        ring_wait(2, 0)
         issue(2, 1)
+    issue(0, 3, 0)
+    issue(1, 3, 0)
+    with jax.named_scope("issue_31"):
+        ring_wait(3, 0)
+    with jax.named_scope("issue_22"):
+        ring_wait(2, 1)
+        issue(2, 2)
+    for which in (0, 1):
+        issue(3, 1, which)
     with jax.named_scope("y_wait"):
         for k in range(1, NY):
             y_wait(k)
             split_rows((y - k + NY) % NY)
-    for m in (0, 1):
-        for ahead in (True, False):
-            ring_wait(m, 3, ahead)
+    with jax.named_scope("wait_03"):
+        for m in (0, 1):
+            ring_wait(m, 3, 0)
     with jax.named_scope("multiply_0"):
         multiply(groups[0], 0, NZ)
     with jax.named_scope("spread_0"):
         pl.semaphore_wait(plane_sem, NY - 1)
         spread_partial(0)
-    with jax.named_scope("issue_31"):
-        issue(3, 1)
-    with jax.named_scope("issue_22"):
-        issue(2, 2)
-    with jax.named_scope("issue_32"):
-        issue(3, 2)
-    multiply(late, 0, 3)
-    with jax.named_scope("issue_23"):
-        issue(2, 3)
+    with jax.named_scope("multiply_1a"):
+        ring_wait(2, 2)
+        multiply(groups[1], 0, 4)
+    with jax.named_scope("issue_320"):
+        ring_wait(3, 1, 0)
+        issue(3, 2, 0)
+        issue(2, 3, 0)
+    with jax.named_scope("multiply_1b"):
+        multiply(groups[1], 5, NZ)
+    with jax.named_scope("issue_321"):
+        ring_wait(3, 1, 1)
+        issue(3, 2, 1)
+    with jax.named_scope("multiply_2"):
+        multiply(groups[2], 0, 3)
+        multiply(groups[2], 6, NZ)
     with jax.named_scope("issue_33"):
-        issue(3, 3)
-    multiply(late, 3, 4)
-    multiply(late, 5, NZ)
+        ring_wait(3, 2, 0)
+        issue(3, 3, 0)
+    with jax.named_scope("wait_23"):
+        ring_wait(2, 3, 0)
+    with jax.named_scope("spread_1"):
+        multiply(groups[1], 4, 5)
+        spread_partial(1)
+    with jax.named_scope("wait_32"):
+        ring_wait(3, 2, 1)
+        multiply(groups[2], 3, 4)
+        multiply(groups[2], 5, 6)
     with jax.named_scope("total_0"):
         total_and_spread(0)
-    for m in (2, 3):
-        with jax.named_scope("last_wait"):
-            for ahead in (True, False):
-                ring_wait(m, 3, ahead)
-        with jax.named_scope("multiply_last"):
-            multiply(groups[m - 1], 4, 5)
-        with jax.named_scope("spread_last"):
-            spread_partial(m - 1)
+    with jax.named_scope("last_wait"):
+        ring_wait(3, 3, 0)
+    with jax.named_scope("spread_2"):
+        multiply(groups[2], 4, 5)
+        spread_partial(2)
     with jax.named_scope("total_1"):
         total_and_spread(1)
     with jax.named_scope("total_2"):
         total_and_spread(2)
+
     side = width // NY
     low = side // 2
     tile = 8
@@ -532,7 +539,7 @@
             pltpu.VMEM((NZ * early, side), F32),
             pltpu.VMEM((NZ * late, side), F32),
             dma((NY - 1,)), dma((NY - 1,)),
-            dma((4, 4)), dma((4, 4)), dma((4, 4)), dma((4, 4)), dma((2,)),
+            dma((4, 6)), dma((4, 6)), dma((4, 6)), dma((4, 6)), dma((2,)),
             dma((3,)), dma((3,)), dma((3,)), dma((3,)),
             dma((2,)), dma((2,)), dma((2,)), dma((2, NY)), dma((2, NY)), dma((2, NY)),
             pltpu.SemaphoreType.REGULAR,

time: 88.4 us -> 87.2 us (0.986)
  Pallas kernels: 87.6 us -> 86.4 us
    pallas_call x1, Pallas kernels: 76.7 us -> 75.6 us  [local(): pl.pallas_call(gather_kernel, name='gather', out_shape=(jax.ShapeDtypeStr...]
where the time goes in v6:
time: 87.2 us; the launch traced here: 87.1 us
  Pallas kernels  86.4 us (99%)
    pallas_call x1, Pallas kernels, local(): pl.pallas_call(gather_kernel, name='gather', out_shape=(jax.ShapeDtypeStr...  75.6 us
    pallas_call x1, Pallas kernels, local(): pl.pallas_call(polar_kernel, name='polar', out_shape=(jax.ShapeDtypeStruc...  10.9 us

profile of v6, /device:TPU:1, one launch (start us, length us, event | category | flops | bytes accessed | tf_op | source)
XLA Modules:
  0.0 87.1 jit_solution(17346684274367676649)
XLA Ops:
  0.6 75.6 %gather.1 = (f32[768,128]{1,0:T(8,128)S(1)}, f32[512,128]{1,0:T(8,128)S(1)}, f32[64,512]{1,0:T(8,128)S(1)}) custom-call(f32[64,8192]{1,0:T(8,128)} %mat_hbm.1, f32[256,512]{1,0:T(8,128)} %bas_hbm.1), custom_call_target="tpu_custom_call" | custom-call | tf_op jit(solution)/shard_map/gather/pallas_call | solution.py:517
  76.2 10.9 %polar.1 = (f32[16,64]{1,0:T(8,128)}, f32[64,512]{1,0:T(8,128)}) custom-call(f32[768,128]{1,0:T(8,128)S(1)} %get-tuple-element.7.packed_early, f32[512,128]{1,0:T(8,128)S(1)} %get-tuple-element.8.packed_late, f32[64,512]{1,0:T(8,128)S(1)} %get-tuple-element.9.own_cols), custom_call_target="tpu_custom_call" | custom-call | tf_op jit(solution)/shard_map/polar/pallas_call | solution.py:551

commit v7 on v6

--- a/solution.py
+++ b/solution.py
@@ -332,31 +332,29 @@
         packed[own, :] = total
         for k in range(PLANE - 1):
             r2, _, c2 = plane_peer(k)
-            if PEERS[k][2] == 0:
+            if turn == 1 or PEERS[k][2] == 0:
+                at = PEERS[k][1] if turn == 0 else 0
                 pltpu.make_async_remote_copy(
                     src_ref=packed.at[own, :], dst_ref=packed.at[own, :],
-                    send_sem=g_send.at[turn], recv_sem=g_recv.at[turn, PEERS[k][1]],
+                    send_sem=g_send.at[turn], recv_sem=g_recv.at[turn, at],
                     device_id=(r2, c2), device_id_type=MESH,
                 ).start()
 
-    def crossing(turn, of_core, ky):
-        packed = rounds[turn][3]
-        at = packed_rows(turn, of_core, (y - ky + NY) % NY, 0, NX)
+    def crossing(of_core, ky):
+        at = packed_rows(0, of_core, (y - ky + NY) % NY, 0, NX)
         return pltpu.make_async_remote_copy(
-            src_ref=packed.at[at, :], dst_ref=packed.at[at, :],
-            send_sem=d_send.at[turn, ky], recv_sem=d_recv.at[turn, ky],
+            src_ref=packed_early.at[at, :], dst_ref=packed_early.at[at, :],
+            send_sem=d_send.at[ky], recv_sem=d_recv.at[ky],
             device_id=partner, device_id_type=MESH,
         )
 
-    def cross(turn):
+    def gram_pieces(turn, pieces, at):
         _, part_of, _, packed = rounds[turn]
-        for ky in (0, 1, 3, 2):
-            view = packed.at[pl.ds(0, (NX - 1 if ky == 0 else NX) * part_of.shape[0]), :]
-            pltpu.make_async_remote_copy(
-                src_ref=view, dst_ref=view, send_sem=g_send.at[turn], recv_sem=g_recv.at[turn, ky],
-                device_id=partner, device_id_type=MESH,
-            ).wait_recv()
-            crossing(turn, core, ky).start()
+        view = packed.at[pl.ds(0, pieces * part_of.shape[0]), :]
+        return pltpu.make_async_remote_copy(
+            src_ref=view, dst_ref=view, send_sem=g_send.at[turn], recv_sem=g_recv.at[turn, at],
+            device_id=partner, device_id_type=MESH,
+        )
 
     with jax.named_scope("proj_wait"):
         for group in range(2):
@@ -372,14 +370,15 @@
     with jax.named_scope("z_wait_late"):
         spread_gram(1)
     with jax.named_scope("cross"):
-        cross(0)
-    with jax.named_scope("cross_late"):
-        cross(1)
+        for ky in (0, 1, 3, 2):
+            gram_pieces(0, NX - 1 if ky == 0 else NX, ky).wait_recv()
+            crossing(core, ky).start()
+    own_cols[...] = proj[lanes(y, cols), :]
     with jax.named_scope("partner_wait"):
-        for turn in range(2):
-            for ky in range(NY):
-                crossing(turn, 1 - core, ky).wait_recv()
-    own_cols[...] = proj[lanes(y, cols), :]
+        for ky in range(NY):
+            crossing(1 - core, ky).wait_recv()
+    with jax.named_scope("late_wait"):
+        gram_pieces(1, PLANE - 1, 0).wait_recv()
 
     with jax.named_scope("send_waits"):
         for copy in copies:
@@ -390,15 +389,11 @@
             all_of(land, group, p_send, p_recv).wait_send()
             all_of(proj, group, a_send, a_recv).wait_send()
         for turn in range(2):
-            _, part_of, _, packed = rounds[turn]
             z_all(turn).wait_send()
-            view = packed.at[pl.ds(0, (NX * NY - 1) * part_of.shape[0]), :]
-            pltpu.make_async_remote_copy(
-                src_ref=view, dst_ref=view, send_sem=g_send.at[turn], recv_sem=g_recv.at[turn, 0],
-                device_id=partner, device_id_type=MESH,
-            ).wait_send()
-            for ky in range(NY):
-                crossing(turn, core, ky).wait_send()
+        gram_pieces(0, NX * NY - 1, 0).wait_send()
+        gram_pieces(1, PLANE - 1, 0).wait_send()
+        for ky in range(NY):
+            crossing(core, ky).wait_send()
 
 
 def polar_kernel(packed_early, packed_late, own_cols, root, right, t, u_hi, u_lo, b_hi, b_lo, v):
@@ -541,7 +536,7 @@
             dma((NY - 1,)), dma((NY - 1,)),
             dma((4, 6)), dma((4, 6)), dma((4, 6)), dma((4, 6)), dma((2,)),
             dma((3,)), dma((3,)), dma((3,)), dma((3,)),
-            dma((2,)), dma((2,)), dma((2,)), dma((2, NY)), dma((2, NY)), dma((2, NY)),
+            dma((2,)), dma((2,)), dma((2,)), dma((2, NY)), dma((NY,)), dma((NY,)),
             pltpu.SemaphoreType.REGULAR,
         ],
         compiler_params=pltpu.CompilerParams(

time: 87.2 us -> 85.9 us (0.985)
  Pallas kernels: 86.4 us -> 85.2 us
    pallas_call x1, Pallas kernels: 75.6 us -> 74.3 us  [local(): pl.pallas_call(gather_kernel, name='gather', out_shape=(jax.ShapeDtypeStr...]
where the time goes in v7:
time: 85.9 us; the launch traced here: 85.8 us
  Pallas kernels  85.2 us (99%)
    pallas_call x1, Pallas kernels, local(): pl.pallas_call(gather_kernel, name='gather', out_shape=(jax.ShapeDtypeStr...  74.3 us
    pallas_call x1, Pallas kernels, local(): pl.pallas_call(polar_kernel, name='polar', out_shape=(jax.ShapeDtypeStruc...  10.9 us

profile of v7, /device:TPU:1, one launch (start us, length us, event | category | flops | bytes accessed | tf_op | source)
XLA Modules:
  0.0 85.8 jit_solution(3126291263683691708)
XLA Ops:
  0.6 74.3 %gather.1 = (f32[768,128]{1,0:T(8,128)S(1)}, f32[512,128]{1,0:T(8,128)S(1)}, f32[64,512]{1,0:T(8,128)S(1)}) custom-call(f32[64,8192]{1,0:T(8,128)} %mat_hbm.1, f32[256,512]{1,0:T(8,128)} %bas_hbm.1), custom_call_target="tpu_custom_call" | custom-call | tf_op jit(solution)/shard_map/gather/pallas_call | solution.py:512
  74.9 10.9 %polar.1 = (f32[16,64]{1,0:T(8,128)}, f32[64,512]{1,0:T(8,128)}) custom-call(f32[768,128]{1,0:T(8,128)S(1)} %get-tuple-element.7.packed_early, f32[512,128]{1,0:T(8,128)S(1)} %get-tuple-element.8.packed_late, f32[64,512]{1,0:T(8,128)S(1)} %get-tuple-element.9.own_cols), custom_call_target="tpu_custom_call" | custom-call | tf_op jit(solution)/shard_map/polar/pallas_call | solution.py:546

commit v8 on v7

--- a/solution.py
+++ b/solution.py
@@ -157,10 +157,11 @@
 
         lax.fori_loop(first, last, one, 0)
 
-    def spread_partial(group):
+    def spread_partial(group, steps=range(NY)):
         here = groups[group]
-
         for k in range(PLANE - 1):
+            if PEERS[k][1] not in steps:
+                continue
             r2, y2, c2 = plane_peer(k)
             src = pl.ds(pl.multiple_of(y2 * cols + r2 * piece, piece), piece)
             pltpu.make_async_remote_copy(
@@ -226,11 +227,13 @@
         for k in range(1, NY):
             y_wait(k)
             split_rows((y - k + NY) % NY)
+    with jax.named_scope("multiply_0"):
+        multiply(groups[0], 0, 4)
+        multiply(groups[0], 5, NZ)
     with jax.named_scope("wait_03"):
         for m in (0, 1):
             ring_wait(m, 3, 0)
-    with jax.named_scope("multiply_0"):
-        multiply(groups[0], 0, NZ)
+        multiply(groups[0], 4, 5)
     with jax.named_scope("spread_0"):
         pl.semaphore_wait(plane_sem, NY - 1)
         spread_partial(0)
@@ -266,8 +269,13 @@
     with jax.named_scope("last_wait"):
         ring_wait(3, 3, 0)
     with jax.named_scope("spread_2"):
-        multiply(groups[2], 4, 5)
-        spread_partial(2)
+        at = lanes((z + 4) % NZ, rows)
+        qh, ql = split(q[at, groups[2]])
+        for steps in ((2,), (1, 3, 0)):
+            for d in steps:
+                own = lanes(near_y[d], cols)
+                acc[own, groups[2]] += product(m_hi[own, at], m_lo[own, at], qh, ql)
+            spread_partial(2, steps)
     with jax.named_scope("total_1"):
         total_and_spread(1)
     with jax.named_scope("total_2"):

time: 85.9 us -> 86 us (level)
  no operation moved by 1% of the time
where the time goes in v8:
time: 86 us; the launch traced here: 85.9 us
  Pallas kernels  85.2 us (99%)
    pallas_call x1, Pallas kernels, local(): pl.pallas_call(gather_kernel, name='gather', out_shape=(jax.ShapeDtypeStr...  74.3 us
    pallas_call x1, Pallas kernels, local(): pl.pallas_call(polar_kernel, name='polar', out_shape=(jax.ShapeDtypeStruc...  10.9 us

profile of v8, /device:TPU:1, one launch (start us, length us, event | category | flops | bytes accessed | tf_op | source)
XLA Modules:
  0.0 85.9 jit_solution(10511400859207944313)
XLA Ops:
  0.6 74.3 %gather.1 = (f32[768,128]{1,0:T(8,128)S(1)}, f32[512,128]{1,0:T(8,128)S(1)}, f32[64,512]{1,0:T(8,128)S(1)}) custom-call(f32[64,8192]{1,0:T(8,128)} %mat_hbm.1, f32[256,512]{1,0:T(8,128)} %bas_hbm.1), custom_call_target="tpu_custom_call" | custom-call | tf_op jit(solution)/shard_map/gather/pallas_call | solution.py:520
  75.0 10.9 %polar.1 = (f32[16,64]{1,0:T(8,128)}, f32[64,512]{1,0:T(8,128)}) custom-call(f32[768,128]{1,0:T(8,128)S(1)} %get-tuple-element.7.packed_early, f32[512,128]{1,0:T(8,128)S(1)} %get-tuple-element.8.packed_late, f32[64,512]{1,0:T(8,128)S(1)} %get-tuple-element.9.own_cols), custom_call_target="tpu_custom_call" | custom-call | tf_op jit(solution)/shard_map/polar/pallas_call | solution.py:554
